TPU v7x, 32 devices: a whole 2x2x4 slice. The times are simulated.
32 devices in a mesh: dp: 4 (over x, y), tp: 8 (over z, core).
Axes of the slice: x: 2, y: 2, z: 4, core: 2. Of those that a mesh axis runs over, the one named last changes fastest.
Arguments:
- x: bfloat16 [256, 3072], P('dp'), parts along dimension 0
- k_cache: bfloat16 [256, 1024, 32, 96], P('dp', None, 'tp'), parts along dimension 0
- v_cache: bfloat16 [256, 1024, 32, 96], P('dp', None, 'tp'), parts along dimension 0
- gain_a: bfloat16 [3072], replicated
- wq: bfloat16 [3072, 3072], P(None, 'tp')
- wo: bfloat16 [3072, 3072], P('tp')
- gain_m: bfloat16 [3072], replicated
- w_gate: bfloat16 [3072, 8192], P(None, 'tp')
- w_up: bfloat16 [3072, 8192], P(None, 'tp')
- w_down: bfloat16 [8192, 3072], P('tp')
Outputs:
- output: bfloat16 [256, 3072], P('dp'), parts along dimension 0
There are 4 independent parts. A program takes and returns all parts, laid end to end along the dimension named above; an argument that names none is the same for every part.
All inputs are finite; a program needn't handle non-finite values.
Results may differ from a plain program's by a relative error of at most 0.017.
Values are sent between devices in bfloat16 or wider.
A program may use at most 2 GiB of HBM per device.

v0:
```python
import jax
import jax.numpy as jnp
from jax import lax
from jax.sharding import PartitionSpec as P

HEAD = 96
THETA = 10000


def normed(x, gain):
    wide = x.astype(jnp.float32)
    scale = lax.rsqrt(jnp.mean(wide * wide, -1, keepdims=True) + 1e-6)
    return (wide * scale * gain.astype(jnp.float32)).astype(jnp.bfloat16)


def turned(t, place, theta):
    half = t.shape[-1] // 2
    angle = place.astype(jnp.float32)[:, None] * theta ** (-jnp.arange(half, dtype=jnp.float32) / half)
    cos, sin = jnp.cos(angle)[:, None], jnp.sin(angle)[:, None]
    a, b = t[..., :half].astype(jnp.float32), t[..., half:].astype(jnp.float32)
    return jnp.concatenate([a * cos - b * sin, b * cos + a * sin], -1).astype(jnp.bfloat16)


def matmul(a, w):
    return jnp.dot(a, w, preferred_element_type=jnp.float32).astype(jnp.bfloat16)


def einsum(form, a, b):
    return jnp.einsum(form, a.astype(jnp.float32), b.astype(jnp.float32))


def seen_by(a, wq, k_cache, v_cache, head, theta):
    batch, cache, kv_heads = k_cache.shape[:3]
    place = jnp.full((batch,), cache - 1)
    q = turned(matmul(a, wq).reshape(batch, -1, head), place, theta).reshape(batch, kv_heads, -1, head)
    scores = einsum("bgsd,bugd->bgsu", q, k_cache) * head**-0.5
    weights = jax.nn.softmax(scores, -1).astype(jnp.bfloat16)
    return einsum("bgsu,bugd->bgsd", weights, v_cache).astype(jnp.bfloat16).reshape(batch, -1)


def hidden_of(b, w_gate, w_up):
    gate = jnp.dot(b, w_gate, preferred_element_type=jnp.float32)
    up = jnp.dot(b, w_up, preferred_element_type=jnp.float32)
    return (jax.nn.silu(gate) * up).astype(jnp.bfloat16)


def solution(mesh):
    def added(t, term):
        return (t.astype(jnp.float32) + lax.psum(term.astype(jnp.bfloat16), "tp").astype(jnp.float32)).astype(jnp.bfloat16)

    def step(x, k_cache, v_cache, gain_a, wq, wo, gain_m, w_gate, w_up, w_down):
        seen = seen_by(normed(x, gain_a), wq, k_cache, v_cache, HEAD, THETA)
        h = added(x, jnp.dot(seen, wo, preferred_element_type=jnp.float32))
        return added(h, jnp.dot(hidden_of(normed(h, gain_m), w_gate, w_up), w_down, preferred_element_type=jnp.float32))

    states, cache, columns, rows_of = P("dp", None), P("dp", None, "tp", None), P(None, "tp"), P("tp", None)
    return jax.shard_map(
        step,
        mesh=mesh,
        in_specs=(states, cache, cache, P(None), columns, rows_of, P(None), columns, columns, rows_of),
        out_specs=states,
        check_vma=False,
    )
```

profile of v0, /device:TPU:0, one launch (start us, length us, event | category | flops | bytes accessed | tf_op | source)
XLA Modules:
  0.0 189.2 jit_solution(4496539789233219556)
XLA Ops:
  6.5 0.0 copy-start
  6.5 0.0 all-reduce.3.cloned.1.call-start
  6.6 0.8 convert_element_type.66
  7.4 1.2 fusion.11
  8.6 2.4 %convolution_convert_fusion.2 = bf16[64,384]{1,0:T(8,128)(2,1)S(1)} fusion(bf16[3072,384]{1,0:T(8,128)(2,1)} %param.14, bf16[64,3072]{1,0:T(8,128)(2,1)} %param.10, f32[3072]{0:T(1024)S(1)} %convert_element_type.66, f32[64]{0:T(128)S(1)} %add_rsqrt_fusion.1), kind=kOutput, calls=%fused_computation.17 | convolution fusion | flops 151805952 | bytes 2814208 | tf_op jit(solution)/shard_map/dot_general | solution.py:25
  11.0 0.1 copy.11
  11.1 0.1 fusion.34
  11.3 0.1 copy.12
  11.4 18.7 %fusion.45 = f32[64,4,1,1024]{3,2,1,0:T(1,128)S(1)} fusion(bf16[64,4,96,1]{2,3,1,0:T(2,128)(2,1)S(1)} %copy.12, bf16[64,1024,4,96]{1,3,2,0:T(8,128)(2,1)} %param.11), kind=kOutput, calls=%fused_computation.58 | convolution fusion | flops 50331648 | bytes 51429376 | tf_op jit(solution)/shard_map/bgsd,bugd->bgsu/dot_general | solution.py:29
  30.1 2.2 %fusion.6 = bf16[64,4,1024,1]{2,0,1,3:T(8,128)(2,1)} fusion(f32[64,4,1,1024]{3,2,1,0:T(1,128)S(1)} %fusion.45), kind=kOutput, calls=%fused_computation.8 | output fusion | flops 1051134 | bytes 1572864 | tf_op jit(solution)/shard_map/div | solution.py:37
  32.3 20.0 %fusion.8 = f32[64,4,1,96]{3,2,1,0:T(1,128)S(1)} fusion(bf16[64,1024,4,96]{1,3,2,0:T(8,128)(2,1)} %param.12, bf16[64,4,1024,1]{2,0,1,3:T(8,128)(2,1)} %fusion.6), kind=kOutput, calls=%fused_computation.19 | convolution fusion | flops 50331648 | bytes 50954240 | tf_op jit(solution)/shard_map/bgsu,bugd->bgsd/dot_general | solution.py:29
  52.3 0.1 reshape.62
  52.5 0.0 copy-done
  52.5 1.3 convolution_convert_fusion.1
  53.7 0.0 all-reduce.3.cloned.1.call-update
  53.8 0.0 all-reduce.5.cloned.1.call-start
  53.8 0.0 copy-done.2
  53.8 58.7 %all-reduce.3.cloned.1.call-done = bf16[64,3072]{1,0:T(8,128)(2,1)} async-done(((bf16[64,3072]{1,0:T(8,128)(2,1)}), bf16[64,3072]{1,0:T(8,128)(2,1)}) %all-reduce.3.cloned.1.call-update) | async-done | bytes 393232 | tf_op jit(solution)/shard_map/psum | solution.py:49
  112.5 1.2 fusion.15
  113.8 4.0 %fusion.31 = f32[64,1024]{1,0:T(8,128)S(1)} fusion(bf16[3072,1024]{1,0:T(8,128)(2,1)} %param.17, bf16[64,3072]{1,0:T(8,128)(2,1)S(1)} %get-tuple-element.6, f32[3072]{0:T(1024)S(1)} %convert_element_type.77, f32[64]{0:T(128)S(1)} %add_rsqrt_fusion), kind=kOutput, calls=%fused_computation.43 | convolution fusion | flops 403439616 | bytes 6959360 | tf_op jit(solution)/shard_map/dot_general | solution.py:42
  117.8 7.7 %convolution_convert_fusion = bf16[64,3072]{1,0:T(8,128)(2,1)} fusion(bf16[1024,3072]{1,0:T(8,128)(2,1)} %param.19, bf16[3072,1024]{1,0:T(8,128)(2,1)} %param.18, f32[64,1024]{1,0:T(8,128)S(1)} %fusion.31, bf16[64,3072]{1,0:T(8,128)(2,1)S(1)} %get-tuple-element.6, f32[3072]{0:T(1024)S(1)} %convert_element_type.77, f32[64]{0:T(128)S(1)} %add_rsqrt_fusion), kind=kOutput, calls=%fused_computation.2 | convolution fusion | flops 806682624 | bytes 13644032 | tf_op jit(solution)/shard_map/dot_general | solution.py:54
  125.5 0.0 all-reduce.5.cloned.1.call-update
  125.6 55.0 %all-reduce.5.cloned.1.call-done = bf16[64,3072]{1,0:T(8,128)(2,1)} async-done(((bf16[64,3072]{1,0:T(8,128)(2,1)}), bf16[64,3072]{1,0:T(8,128)(2,1)}) %all-reduce.5.cloned.1.call-update) | async-done | bytes 393232 | tf_op jit(solution)/shard_map/psum | solution.py:49
  180.5 1.8 fusion.18
  (9 shorter events, 0.1 us)
Async XLA Ops:
  6.5 45.9 %copy-start = (bf16[384,3072]{1,0:T(8,128)(2,1)S(1)}, bf16[384,3072]{1,0:T(8,128)(2,1)}, u32[]{:S(2)}) copy-start(bf16[384,3072]{1,0:T(8,128)(2,1)} %param.15) | copy-start | bytes 7077892
  6.5 106.0 %all-reduce.3.cloned.1.call-start = ((), (), s32[]{:S(2)}) async-start(), calls=%async_computation | async-start | bytes 786432 | tf_op jit(solution)/shard_map/psum | solution.py:49
  32.3 21.5 %copy-start.2 = (bf16[3072]{0:T(1024)(128)(2,1)S(1)}, bf16[3072]{0:T(1024)(128)(2,1)}, u32[]{:S(2)}) copy-start(bf16[3072]{0:T(1024)(128)(2,1)} %param.16) | copy-start | bytes 18436
  32.3 80.2 %copy-start.1 = (bf16[64,3072]{1,0:T(8,128)(2,1)S(1)}, bf16[64,3072]{1,0:T(8,128)(2,1)}, u32[]{:S(2)}) copy-start(bf16[64,3072]{1,0:T(8,128)(2,1)} %param.10) | copy-start | bytes 1179652
  53.8 126.8 %all-reduce.5.cloned.1.call-start = ((), (), s32[]{:S(2)}) async-start(), calls=%async_computation.1 | async-start | bytes 786432 | tf_op jit(solution)/shard_map/psum | solution.py:49
Sparse Core Ops, SparseCore 0:
  53.9 58.5 all-reduce.2
  125.7 54.8 all-reduce.4
where the time goes:
time: 190 us; the launch traced here: 189 us
  waiting for transfers between devices  114 us (60%)
  matrix products  54.1 us (28%)
  between operations  13.5 us (7%)
  other arithmetic  7.52 us (4%)
    psum x2, waiting for transfers between devices, added(): lax.psum(term.astype(jnp.bfloat16), 'tp').astype(jnp.float32)  114 us
    dot_general x2, matrix products, einsum(): return jnp.einsum(form, a.astype(jnp.float32), b.astype(jnp.float32))  38.7 us
    dot_general x1, matrix products, step(): jnp.dot(hidden_of(normed(h, gain_m), w_gate, w_up), w_down, preferred_ele...  7.72 us
    dot_general x1, matrix products, hidden_of(): gate = jnp.dot(b, w_gate, preferred_element_type=jnp.float32)  4.05 us
  transfers between devices with their start and end apart: 2, of which 2 were waited for; matrix products, arithmetic and copies ran while one was open for 0% of the time, Pallas kernels for 0%

commit v1 on v0

v1 whole, which is shorter than its diff:
```python
import functools

import jax
import jax.numpy as jnp
import numpy as np
from jax import lax
from jax.experimental import pallas as pl
from jax.experimental.pallas import tpu as pltpu
from jax.sharding import PartitionSpec as P

HEAD = 96
THETA = 10000
N = 8
ROWS, D = 64, 3072
COLS = D // N
HEADS = 4
QD = HEADS * HEAD
CACHE = 1024
FF = 1024
SEQS = 4
CHUNKS = ROWS // SEQS
SLOTS = 4
GROUP = 16
GROUPS = ROWS // GROUP
PER = GROUP // SEQS
MTILE = 256
F32, BF16 = jnp.float32, jnp.bfloat16


def dot(a, b):
    return jnp.dot(a, b, preferred_element_type=F32)


def kernel(x_h, k_h, v_h, ga_h, wq_h, wo_h, gm_h, wg_h, wu_h, wd_h, cs_h, out_h,
           x_v, ga_v, gm_v, cs_v, wq_v, wo_v, wg_v, wu_v, wd_v, k_v, v_v,
           a_v, q_s, p_s, seen_s, term_s, tsend, trecv, h_v, hid_v, ysend, yrecv, y_v,
           in_sem, k_sem, v_sem, w_sem, out_sem, rs_s, rs_r, ag_s, ag_r, rs2_s, rs2_r, ag2_s, ag2_r):
    me = lax.axis_index("tp")

    def peer(k):
        return lax.rem(me + k, N)

    def local(src, dst, sem):
        return pltpu.make_async_copy(src, dst, sem)

    x_in = local(x_h, x_v, in_sem.at[0])
    ga_in = local(ga_h, ga_v, in_sem.at[1])
    cs_in = local(cs_h, cs_v, in_sem.at[2])
    wq_in = local(wq_h, wq_v, in_sem.at[3])
    wo_in = local(wo_h, wo_v, in_sem.at[4])
    gm_in = local(gm_h, gm_v, in_sem.at[5])

    def k_in(c):
        s = lax.rem(c, SLOTS)
        return local(k_h.at[c], k_v.at[s], k_sem.at[s])

    def v_in(c):
        s = lax.rem(c, SLOTS)
        return local(v_h.at[c], v_v.at[s], v_sem.at[s])

    def w_in(n):
        cols = pl.ds(n * MTILE, MTILE)
        return (local(wg_h.at[:, cols], wg_v.at[:, cols], w_sem.at[0, n]),
                local(wu_h.at[:, cols], wu_v.at[:, cols], w_sem.at[1, n]))

    wd_in = local(wd_h, wd_v, in_sem.at[6])

    x_in.start()
    ga_in.start()
    cs_in.start()
    wq_in.start()
    for c in range(SLOTS):
        k_in(c).start()
        v_in(c).start()
        if c == 0:
            wo_in.start()
            gm_in.start()

    barrier = pltpu.get_barrier_semaphore()
    for k in range(1, N):
        pl.semaphore_signal(barrier, inc=1, device_id={"tp": peer(k)}, device_id_type=pl.DeviceIdType.MESH)
    pl.semaphore_wait(barrier, N - 1)

    x_in.wait()
    ga_in.wait()

    def norm_x(i, _):
        rows = pl.ds(pl.multiple_of(i * GROUP, GROUP), GROUP)
        wide = x_v[rows, :].astype(F32)
        scale = lax.rsqrt(jnp.mean(wide * wide, -1, keepdims=True) + 1e-6)
        a_v[rows, :] = (wide * scale * ga_v[...].astype(F32)).astype(BF16)
        return 0

    lax.fori_loop(0, GROUPS, norm_x, 0)
    wq_in.wait()
    cs_in.wait()
    q = dot(a_v[...], wq_v[...]).astype(BF16).astype(F32)
    lane = lax.broadcasted_iota(jnp.int32, (ROWS, QD), 1)
    ahead = pltpu.roll(q, QD - HEAD // 2, 1)
    behind = pltpu.roll(q, HEAD // 2, 1)
    turn = jnp.where(lax.rem(lane, HEAD) < HEAD // 2, -ahead, behind)
    q_s[...] = (q * cs_v[0:1, :] + turn * cs_v[1:2, :]).astype(BF16).astype(F32)

    row16 = lax.broadcasted_iota(jnp.int32, (SEQS * HEADS, QD), 0)
    lane16 = lax.broadcasted_iota(jnp.int32, (SEQS * HEADS, QD), 1)
    masks = [row16 == i * HEADS + lane16 // HEAD for i in range(SEQS)]

    def weights_of(c):
        k_in(c).wait()
        parts = []
        for i in range(SEQS):
            row = q_s[pl.ds(c * SEQS + i, 1), :]
            parts.append(jnp.where(masks[i], jnp.broadcast_to(row, (SEQS * HEADS, QD)), 0.0))
        qd = jnp.concatenate(parts, 1).astype(BF16)
        s = dot(qd, k_v[lax.rem(c, SLOTS)]) * HEAD**-0.5
        e = jnp.exp(s - jnp.max(s, -1, keepdims=True))
        return (e * (1.0 / jnp.sum(e, -1, keepdims=True))).astype(BF16)

    def values_of(c, p):
        o = lax.dot_general(p, v_v[lax.rem(c, SLOTS)], (((1,), (1,)), ((), ())), preferred_element_type=F32)
        for i in range(SEQS):
            part = jnp.where(masks[i], o[:, i * QD:(i + 1) * QD], 0.0)
            seen_s[pl.ds(c * SEQS + i, 1), :] = jnp.sum(part, 0, keepdims=True)

    def group_rows(g):
        return pl.ds(pl.multiple_of(g * GROUP, GROUP), GROUP)

    def rs_copy(g, k):
        return pltpu.make_async_remote_copy(
            src_ref=tsend.at[g, peer(k)], dst_ref=trecv.at[g, k], send_sem=rs_s.at[g, k], recv_sem=rs_r.at[g, k],
            device_id={"tp": peer(k)}, device_id_type=pl.DeviceIdType.MESH)

    def ag_copy(g, k):
        block = h_v.at[me, group_rows(g), :]
        return pltpu.make_async_remote_copy(
            src_ref=block, dst_ref=block, send_sem=ag_s.at[g, k], recv_sem=ag_r.at[g, k],
            device_id={"tp": peer(k)}, device_id_type=pl.DeviceIdType.MESH)

    def send_terms(g):
        seen = seen_s[group_rows(g), :].astype(BF16)
        term = dot(seen, wo_v[...])
        for j in range(N):
            block = term[:, j * COLS:(j + 1) * COLS]
            term_s[g, j] = block
            tsend[g, j] = block.astype(BF16)
        for k in range(1, N):
            rs_copy(g, k).start()

    def finish_h(g):
        rows = group_rows(g)
        total = term_s[g, me]
        for k in range(1, N):
            rs_copy(g, k).wait_recv()
            total = total + trecv[g, k].astype(F32)
        mine = x_v[rows, pl.ds(pl.multiple_of(me * COLS, COLS), COLS)].astype(F32)
        h_v[me, rows, :] = (mine + total).astype(BF16)
        for k in range(1, N):
            ag_copy(g, k).start()

    def norm_h(g):
        rows = group_rows(g)
        for k in range(1, N):
            ag_copy(g, k).wait_recv()
        wide = [h_v[j, rows, :].astype(F32) for j in range(N)]
        square = sum(jnp.sum(w * w, -1, keepdims=True) for w in wide)
        scale = lax.rsqrt(square / D + 1e-6)
        for j in range(N):
            cols = slice(j * COLS, (j + 1) * COLS)
            a_v[rows, cols] = (wide[j] * scale * gm_v[:, cols].astype(F32)).astype(BF16)

    p_s[...] = weights_of(0)
    wo_in.wait()
    gm_in.wait()

    def chunk(c, _):
        @pl.when(c + SLOTS - 1 < CHUNKS)
        def _():
            k_in(c + SLOTS - 1).start()

        @pl.when(jnp.logical_and(c >= 2, c + SLOTS - 2 < CHUNKS))
        def _():
            v_in(c + SLOTS - 2).start()

        @pl.when(c == CHUNKS - SLOTS + 1)
        def _():
            for n in range(FF // MTILE):
                for w in w_in(n):
                    w.start()
            wd_in.start()

        v_in(c - 1).wait()
        p = p_s[...]
        p_s[...] = weights_of(c)
        values_of(c - 1, p)

        @pl.when(lax.rem(c, PER) == 0)
        def _():
            send_terms(c // PER - 1)

        @pl.when(jnp.logical_and(lax.rem(c, PER) == PER - 1, c >= 2 * PER - 1))
        def _():
            finish_h(c // PER - 1)

        return 0

    lax.fori_loop(1, CHUNKS, chunk, 0)
    v_in(CHUNKS - 1).wait()
    values_of(CHUNKS - 1, p_s[...])
    send_terms(GROUPS - 1)
    lax.fori_loop(0, GROUPS - 1, lambda g, _: (norm_h(g), 0)[1], 0)
    finish_h(GROUPS - 1)
    norm_h(GROUPS - 1)

    def hidden(n, _):
        for w in w_in(n):
            w.wait()
        cols = pl.ds(pl.multiple_of(n * MTILE, MTILE), MTILE)
        gate = dot(a_v[...], wg_v[:, cols])
        up = dot(a_v[...], wu_v[:, cols])
        hid_v[:, cols] = (jax.nn.silu(gate) * up).astype(BF16)
        return 0

    lax.fori_loop(0, FF // MTILE, hidden, 0)
    wd_in.wait()

    def rs2_copy(k):
        return pltpu.make_async_remote_copy(
            src_ref=ysend.at[k], dst_ref=yrecv.at[k], send_sem=rs2_s.at[k], recv_sem=rs2_r.at[k],
            device_id={"tp": peer(k)}, device_id_type=pl.DeviceIdType.MESH)

    def ag2_copy(k):
        return pltpu.make_async_remote_copy(
            src_ref=y_v.at[me], dst_ref=y_v.at[me], send_sem=ag2_s.at[k], recv_sem=ag2_r.at[k],
            device_id={"tp": peer(k)}, device_id_type=pl.DeviceIdType.MESH)

    def down(j):
        return dot(hid_v[...], wd_v[:, pl.ds(pl.multiple_of(j * COLS, COLS), COLS)])

    for k in range(1, N):
        ysend[k] = down(peer(k)).astype(BF16)
        rs2_copy(k).start()
    total = down(me)
    for k in range(1, N):
        rs2_copy(k).wait_recv()
        total = total + yrecv[k].astype(F32)
    y_v[me] = (h_v[me].astype(F32) + total).astype(BF16)
    for k in range(1, N):
        ag2_copy(k).start()

    def out_copy(j):
        return local(y_v.at[j], out_h.at[:, pl.ds(pl.multiple_of(j * COLS, COLS), COLS)], out_sem.at[j])

    out_copy(me).start()
    for k in range(1, N):
        ag2_copy(k).wait_recv()
        out_copy(lax.rem(me + N - k, N)).start()
    for j in range(N):
        out_copy(j).wait()

    def sent(g, _):
        for k in range(1, N):
            rs_copy(g, k).wait_send()
            ag_copy(g, k).wait_send()
        return 0

    lax.fori_loop(0, GROUPS, sent, 0)
    for k in range(1, N):
        rs2_copy(k).wait_send()
        ag2_copy(k).wait_send()


def turns():
    half = HEAD // 2
    angle = (CACHE - 1) * np.float64(THETA) ** (-np.arange(half) / half)
    table = np.stack([np.cos(angle), np.sin(angle)]).astype(np.float32)
    return np.tile(table, (1, 2 * HEADS))


def solution(mesh):
    dma = pltpu.SemaphoreType.DMA

    def step(x, k_cache, v_cache, gain_a, wq, wo, gain_m, w_gate, w_up, w_down):
        k = k_cache.transpose(0, 2, 3, 1).reshape(CHUNKS, SEQS * QD, CACHE)
        v = v_cache.transpose(0, 2, 3, 1).reshape(CHUNKS, SEQS * QD, CACHE)
        vm = pltpu.VMEM
        return pl.pallas_call(
            kernel,
            out_shape=jax.ShapeDtypeStruct((ROWS, D), BF16),
            in_specs=[pl.BlockSpec(memory_space=pl.ANY)] * 11,
            out_specs=pl.BlockSpec(memory_space=pl.ANY),
            scratch_shapes=[
                vm((ROWS, D), BF16), vm((1, D), BF16), vm((1, D), BF16), vm((2, QD), F32),
                vm((D, QD), BF16), vm((QD, D), BF16), vm((D, FF), BF16), vm((D, FF), BF16), vm((FF, D), BF16),
                vm((SLOTS, SEQS * QD, CACHE), BF16), vm((SLOTS, SEQS * QD, CACHE), BF16),
                vm((ROWS, D), BF16), vm((ROWS, QD), F32), vm((SEQS * HEADS, CACHE), BF16), vm((ROWS, QD), F32),
                vm((GROUPS, N, GROUP, COLS), F32), vm((GROUPS, N, GROUP, COLS), BF16), vm((GROUPS, N, GROUP, COLS), BF16),
                vm((N, ROWS, COLS), BF16), vm((ROWS, FF), BF16),
                vm((N, ROWS, COLS), BF16), vm((N, ROWS, COLS), BF16), vm((N, ROWS, COLS), BF16),
                dma((7,)), dma((SLOTS,)), dma((SLOTS,)), dma((2, FF // MTILE)), dma((N,)),
                dma((GROUPS, N)), dma((GROUPS, N)), dma((GROUPS, N)), dma((GROUPS, N)),
                dma((N,)), dma((N,)), dma((N,)), dma((N,)),
            ],
            compiler_params=pltpu.CompilerParams(collective_id=0, has_side_effects=True, vmem_limit_bytes=66_000_000),
            name="layer",
        )(x, k, v, gain_a.reshape(1, D), wq, wo, gain_m.reshape(1, D), w_gate, w_up, w_down, jnp.asarray(turns()))

    states, cache, columns, rows_of = P("dp", None), P("dp", None, "tp", None), P(None, "tp"), P("tp", None)
    return jax.shard_map(
        step,
        mesh=mesh,
        in_specs=(states, cache, cache, P(None), columns, rows_of, P(None), columns, columns, rows_of),
        out_specs=states,
        check_vma=False,
    )
```

time: 190 us -> 75.4 us (0.40)
  the two profiles are of different devices: /device:TPU:0 before, /device:TPU:27 now
where the time goes in v1:
time: 75.4 us; the launch traced here: 75.1 us
  Pallas kernels  70.7 us (94%)
  local copies, waits for them, and re-layouts  4.36 us (6%)
    pallas_call x1, Pallas kernels, step(): pl.pallas_call(kernel, out_shape=jax.ShapeDtypeStruct((ROWS, D), BF16), i...  70.7 us
    unnamed x1, local copies, waits for them, and re-layouts  1.77 us

profile of v1, /device:TPU:27, one launch (start us, length us, event | category | flops | bytes accessed | tf_op | source)
XLA Modules:
  0.0 75.1 jit_solution(12611721134919099906)
XLA Ops:
  0.0 1.3 %reshape.14.ga_h = bf16[1,3072]{1,0:T(2,128)(2,1)} reshape(bf16[3072]{0:T(1024)(128)(2,1)} %param.14) | data formatting | bytes 12288 | tf_op jit(solution)/shard_map/reshape | solution.py:305
  1.3 1.3 %reshape.15.gm_h = bf16[1,3072]{1,0:T(2,128)(2,1)} reshape(bf16[3072]{0:T(1024)(128)(2,1)} %param.17) | data formatting | bytes 12288 | tf_op jit(solution)/shard_map/reshape | solution.py:305
  2.6 70.7 %layer.1 = bf16[64,3072]{1,0:T(8,128)(2,1)} custom-call(bf16[64,3072]{1,0:T(8,128)(2,1)} %x_h.1, bf16[16,1536,1024]{2,1,0:T(8,128)(2,1)} %bitcast.6, bf16[16,1536,1024]{2,1,0:T(8,128)(2,1)} %bitcast.7, bf16[1,3072]{1,0:T(2,128)(2,1)} %reshape.14.ga_h, bf16[3072,384]{1,0:T(8,128)(2,1)} %wq_h.1, bf16[384,3072]{1,0:T(8,128)(2,1)} %wo_h.1, ...), custom_call_target="tpu_custom_call" | custom-call | tf_op jit(solution)/shard_map/layer/pallas_call | solution.py:286
  73.4 1.8 %copy.13 = bf16[64,3072]{1,0:T(8,128)(2,1)} copy(bf16[64,3072]{1,0:T(8,128)(2,1)} %layer.1) | data formatting | bytes 786432

commit v2 on v1

--- a/solution.py
+++ b/solution.py
@@ -11,6 +11,7 @@
 HEAD = 96
 THETA = 10000
 N = 8
+CHIPS = N // 2
 ROWS, D = 64, 3072
 COLS = D // N
 HEADS = 4
@@ -22,8 +23,12 @@
 SLOTS = 4
 GROUP = 16
 GROUPS = ROWS // GROUP
+EARLY = GROUPS - 1
+HALF = GROUP // 2
 PER = GROUP // SEQS
 MTILE = 256
+PARTS = 2
+PART = ROWS // PARTS
 F32, BF16 = jnp.float32, jnp.bfloat16
 
 
@@ -31,14 +36,32 @@
     return jnp.dot(a, b, preferred_element_type=F32)
 
 
+def gain_of(ref, start, size):
+    rows = range(start // 128, (start + size) // 128)
+    return jnp.concatenate([ref[i:i + 1, :].astype(F32) for i in rows], 1)
+
+
 def kernel(x_h, k_h, v_h, ga_h, wq_h, wo_h, gm_h, wg_h, wu_h, wd_h, cs_h, out_h,
            x_v, ga_v, gm_v, cs_v, wq_v, wo_v, wg_v, wu_v, wd_v, k_v, v_v,
-           a_v, q_s, p_s, seen_s, term_s, tsend, trecv, h_v, hid_v, ysend, yrecv, y_v,
-           in_sem, k_sem, v_sem, w_sem, out_sem, rs_s, rs_r, ag_s, ag_r, rs2_s, rs2_r, ag2_s, ag2_r):
+           a_v, q_s, p_s, seen_s, term_s, tsend, trecv, psend, precv, chips, h_v, hid_v,
+           ysend, yrecv, yown, ysum, yfar, y_v,
+           in_sem, k_sem, v_sem, w_sem, rs_s, rs_r, ag_s, ag_r, pair_s, pair_r, chip_s, chip_r,
+           in2_s, in2_r, rs2_s, rs2_r, ag2_s, ag2_r, out2_s, out2_r):
     me = lax.axis_index("tp")
+
+    z, core = me // 2, lax.rem(me, 2)
+    partner = 2 * z + 1 - core
 
     def peer(k):
         return lax.rem(me + k, N)
+
+    def chip(k):
+        return lax.rem(z + k, CHIPS)
+
+    def remote(src, dst, send_sem, recv_sem, target):
+        return pltpu.make_async_remote_copy(
+            src_ref=src, dst_ref=dst, send_sem=send_sem, recv_sem=recv_sem,
+            device_id={"tp": target}, device_id_type=pl.DeviceIdType.MESH)
 
     def local(src, dst, sem):
         return pltpu.make_async_copy(src, dst, sem)
@@ -88,7 +111,7 @@
         rows = pl.ds(pl.multiple_of(i * GROUP, GROUP), GROUP)
         wide = x_v[rows, :].astype(F32)
         scale = lax.rsqrt(jnp.mean(wide * wide, -1, keepdims=True) + 1e-6)
-        a_v[rows, :] = (wide * scale * ga_v[...].astype(F32)).astype(BF16)
+        a_v[rows, :] = (wide * scale * gain_of(ga_v, 0, D)).astype(BF16)
         return 0
 
     lax.fori_loop(0, GROUPS, norm_x, 0)
@@ -126,15 +149,11 @@
         return pl.ds(pl.multiple_of(g * GROUP, GROUP), GROUP)
 
     def rs_copy(g, k):
-        return pltpu.make_async_remote_copy(
-            src_ref=tsend.at[g, peer(k)], dst_ref=trecv.at[g, k], send_sem=rs_s.at[g, k], recv_sem=rs_r.at[g, k],
-            device_id={"tp": peer(k)}, device_id_type=pl.DeviceIdType.MESH)
+        return remote(tsend.at[g, peer(k)], trecv.at[g, k], rs_s.at[g, k], rs_r.at[g, k], peer(k))
 
     def ag_copy(g, k):
         block = h_v.at[me, group_rows(g), :]
-        return pltpu.make_async_remote_copy(
-            src_ref=block, dst_ref=block, send_sem=ag_s.at[g, k], recv_sem=ag_r.at[g, k],
-            device_id={"tp": peer(k)}, device_id_type=pl.DeviceIdType.MESH)
+        return remote(block, block, ag_s.at[g, k], ag_r.at[g, k], peer(k))
 
     def send_terms(g):
         seen = seen_s[group_rows(g), :].astype(BF16)
@@ -157,16 +176,52 @@
         for k in range(1, N):
             ag_copy(g, k).start()
 
-    def norm_h(g):
-        rows = group_rows(g)
-        for k in range(1, N):
-            ag_copy(g, k).wait_recv()
+    def norm_h(rows):
         wide = [h_v[j, rows, :].astype(F32) for j in range(N)]
         square = sum(jnp.sum(w * w, -1, keepdims=True) for w in wide)
         scale = lax.rsqrt(square / D + 1e-6)
         for j in range(N):
             cols = slice(j * COLS, (j + 1) * COLS)
-            a_v[rows, cols] = (wide[j] * scale * gm_v[:, cols].astype(F32)).astype(BF16)
+            a_v[rows, cols] = (wide[j] * scale * gain_of(gm_v, j * COLS, COLS)).astype(BF16)
+
+    def early_h(g, _):
+        for k in range(1, N):
+            ag_copy(g, k).wait_recv()
+        norm_h(group_rows(g))
+        return 0
+
+    def pair_copy(t):
+        return remote(psend.at[t], precv.at[t], pair_s.at[t], pair_r.at[t], partner)
+
+    def chip_copy(t, k, to, source):
+        part = pl.ds(source * CHIPS, CHIPS)
+        return remote(chips.at[t, 0, part], chips.at[t, k, part], chip_s.at[t, k, to], chip_r.at[t, k, source], 2 * chip(k) + to)
+
+    def late_rows(t):
+        return pl.ds(EARLY * GROUP + t * HALF, HALF)
+
+    def send_pair(t):
+        term = dot(seen_s[late_rows(t), :].astype(BF16), wo_v[...])
+        for j in range(N):
+            psend[t, j] = term[:, j * COLS:(j + 1) * COLS].astype(BF16)
+        pair_copy(t).start()
+
+    def send_chip(t):
+        pair_copy(t).wait_recv()
+        chips[t, 0] = (psend[t].astype(F32) + precv[t].astype(F32)).astype(BF16)
+        for k in (2, 1, 3):
+            for to in range(2):
+                chip_copy(t, k, to, core).start()
+
+    def late_h(t):
+        for k in range(1, CHIPS):
+            for source in range(2):
+                chip_copy(t, k, 0, source).wait_recv()
+        for j in range(N):
+            total = x_v[late_rows(t), j * COLS:(j + 1) * COLS].astype(F32)
+            for q in range(CHIPS):
+                total = total + chips[t, lax.rem(z - q + CHIPS, CHIPS), j].astype(F32)
+            h_v[j, late_rows(t), :] = total.astype(BF16)
 
     p_s[...] = weights_of(0)
     wo_in.wait()
@@ -197,6 +252,14 @@
         def _():
             send_terms(c // PER - 1)
 
+        @pl.when(c == CHUNKS - 2)
+        def _():
+            send_pair(0)
+
+        @pl.when(c == CHUNKS - 1)
+        def _():
+            send_chip(0)
+
         @pl.when(jnp.logical_and(lax.rem(c, PER) == PER - 1, c >= 2 * PER - 1))
         def _():
             finish_h(c // PER - 1)
@@ -206,10 +269,12 @@
     lax.fori_loop(1, CHUNKS, chunk, 0)
     v_in(CHUNKS - 1).wait()
     values_of(CHUNKS - 1, p_s[...])
-    send_terms(GROUPS - 1)
-    lax.fori_loop(0, GROUPS - 1, lambda g, _: (norm_h(g), 0)[1], 0)
-    finish_h(GROUPS - 1)
-    norm_h(GROUPS - 1)
+    send_pair(1)
+    late_h(0)
+    send_chip(1)
+    lax.fori_loop(0, EARLY, early_h, 0)
+    late_h(1)
+    norm_h(group_rows(EARLY))
 
     def hidden(n, _):
         for w in w_in(n):
@@ -223,39 +288,65 @@
     lax.fori_loop(0, FF // MTILE, hidden, 0)
     wd_in.wait()
 
-    def rs2_copy(k):
-        return pltpu.make_async_remote_copy(
-            src_ref=ysend.at[k], dst_ref=yrecv.at[k], send_sem=rs2_s.at[k], recv_sem=rs2_r.at[k],
-            device_id={"tp": peer(k)}, device_id_type=pl.DeviceIdType.MESH)
-
-    def ag2_copy(k):
-        return pltpu.make_async_remote_copy(
-            src_ref=y_v.at[me], dst_ref=y_v.at[me], send_sem=ag2_s.at[k], recv_sem=ag2_r.at[k],
-            device_id={"tp": peer(k)}, device_id_type=pl.DeviceIdType.MESH)
-
-    def down(j):
-        return dot(hid_v[...], wd_v[:, pl.ds(pl.multiple_of(j * COLS, COLS), COLS)])
-
-    for k in range(1, N):
-        ysend[k] = down(peer(k)).astype(BF16)
-        rs2_copy(k).start()
-    total = down(me)
-    for k in range(1, N):
-        rs2_copy(k).wait_recv()
-        total = total + yrecv[k].astype(F32)
-    y_v[me] = (h_v[me].astype(F32) + total).astype(BF16)
-    for k in range(1, N):
-        ag2_copy(k).start()
-
-    def out_copy(j):
-        return local(y_v.at[j], out_h.at[:, pl.ds(pl.multiple_of(j * COLS, COLS), COLS)], out_sem.at[j])
-
-    out_copy(me).start()
-    for k in range(1, N):
-        ag2_copy(k).wait_recv()
-        out_copy(lax.rem(me + N - k, N)).start()
+    def in2(q):
+        return remote(ysend.at[q], yrecv.at[q], in2_s.at[q], in2_r.at[q], partner)
+
+    def part_rows(r):
+        return pl.ds(r * PART, PART)
+
+    def rs2(r, k):
+        return remote(ysum.at[chip(k), part_rows(r)], yfar.at[k, part_rows(r)], rs2_s.at[r, k], rs2_r.at[r, k], 2 * chip(k) + core)
+
+    mine = core * CHIPS + z
+
+    def ag2(r, k, block):
+        b = y_v.at[block, part_rows(r)]
+        return remote(b, b, ag2_s.at[r, k], ag2_r.at[r, k], partner if k == 0 else 2 * chip(k) + core)
+
+    def out2(r, k, block):
+        b = y_v.at[block, part_rows(r)]
+        return remote(b, b, out2_s.at[r, k], out2_r.at[r, k], partner)
+
+    def down(half):
+        return dot(hid_v[...], wd_v[:, pl.ds(pl.multiple_of(half * CHIPS * COLS, CHIPS * COLS), CHIPS * COLS)])
+
+    theirs = down(1 - core)
+    for q in range(CHIPS):
+        ysend[q] = theirs[:, q * COLS:(q + 1) * COLS].astype(BF16)
+    for k in (2, 1, 3, 0):
+        in2(chip(k)).start()
+    ours = down(core)
+    for q in range(CHIPS):
+        yown[q] = ours[:, q * COLS:(q + 1) * COLS]
+    for k in (2, 1, 3):
+        q = chip(k)
+        in2(q).wait_recv()
+        ysum[q] = (yown[q] + yrecv[q].astype(F32)).astype(BF16)
+        rs2(0, k).start()
+    for r in range(1, PARTS):
+        for k in (2, 1, 3):
+            rs2(r, k).start()
+    in2(z).wait_recv()
+    for r in range(PARTS):
+        rows = part_rows(r)
+        total = yown[z, rows, :] + yrecv[z, rows, :].astype(F32)
+        for k in range(1, CHIPS):
+            rs2(r, k).wait_recv()
+            total = total + yfar[k, rows, :].astype(F32)
+        y_v[mine, rows, :] = (h_v[mine, rows, :].astype(F32) + total).astype(BF16)
+        for k in (2, 1, 3, 0):
+            ag2(r, k, mine).start()
+    for r in range(PARTS):
+        for k in (1, 3, 2):
+            block = core * CHIPS + chip(CHIPS - k)
+            ag2(r, k, block).wait_recv()
+            out2(r, k, block).start()
+    for r in range(PARTS):
+        ag2(r, 0, mine).wait_recv()
+        for k in range(1, CHIPS):
+            out2(r, k, mine).wait_recv()
     for j in range(N):
-        out_copy(j).wait()
+        out_h[:, j * COLS:(j + 1) * COLS] = y_v[j]
 
     def sent(g, _):
         for k in range(1, N):
@@ -263,10 +354,20 @@
             ag_copy(g, k).wait_send()
         return 0
 
-    lax.fori_loop(0, GROUPS, sent, 0)
-    for k in range(1, N):
-        rs2_copy(k).wait_send()
-        ag2_copy(k).wait_send()
+    lax.fori_loop(0, EARLY, sent, 0)
+    for t in range(2):
+        pair_copy(t).wait_send()
+        for k in range(1, CHIPS):
+            for to in range(2):
+                chip_copy(t, k, to, core).wait_send()
+    for q in range(CHIPS):
+        in2(q).wait_send()
+    for r in range(PARTS):
+        ag2(r, 0, mine).wait_send()
+        for k in range(1, CHIPS):
+            rs2(r, k).wait_send()
+            ag2(r, k, mine).wait_send()
+            out2(r, k, mine).wait_send()
 
 
 def turns():
@@ -285,24 +386,28 @@
         vm = pltpu.VMEM
         return pl.pallas_call(
             kernel,
-            out_shape=jax.ShapeDtypeStruct((ROWS, D), BF16),
+            out_shape=pltpu.VMEM((ROWS, D), BF16),
             in_specs=[pl.BlockSpec(memory_space=pl.ANY)] * 11,
-            out_specs=pl.BlockSpec(memory_space=pl.ANY),
+            out_specs=pl.BlockSpec(memory_space=pltpu.VMEM),
             scratch_shapes=[
-                vm((ROWS, D), BF16), vm((1, D), BF16), vm((1, D), BF16), vm((2, QD), F32),
+                vm((ROWS, D), BF16), vm((24, 128), BF16), vm((24, 128), BF16), vm((2, QD), F32),
                 vm((D, QD), BF16), vm((QD, D), BF16), vm((D, FF), BF16), vm((D, FF), BF16), vm((FF, D), BF16),
                 vm((SLOTS, SEQS * QD, CACHE), BF16), vm((SLOTS, SEQS * QD, CACHE), BF16),
                 vm((ROWS, D), BF16), vm((ROWS, QD), F32), vm((SEQS * HEADS, CACHE), BF16), vm((ROWS, QD), F32),
-                vm((GROUPS, N, GROUP, COLS), F32), vm((GROUPS, N, GROUP, COLS), BF16), vm((GROUPS, N, GROUP, COLS), BF16),
+                vm((EARLY, N, GROUP, COLS), F32), vm((EARLY, N, GROUP, COLS), BF16), vm((EARLY, N, GROUP, COLS), BF16),
+                vm((2, N, HALF, COLS), BF16), vm((2, N, HALF, COLS), BF16), vm((2, CHIPS, N, HALF, COLS), BF16),
                 vm((N, ROWS, COLS), BF16), vm((ROWS, FF), BF16),
-                vm((N, ROWS, COLS), BF16), vm((N, ROWS, COLS), BF16), vm((N, ROWS, COLS), BF16),
-                dma((7,)), dma((SLOTS,)), dma((SLOTS,)), dma((2, FF // MTILE)), dma((N,)),
-                dma((GROUPS, N)), dma((GROUPS, N)), dma((GROUPS, N)), dma((GROUPS, N)),
-                dma((N,)), dma((N,)), dma((N,)), dma((N,)),
+                vm((CHIPS, ROWS, COLS), BF16), vm((CHIPS, ROWS, COLS), BF16), vm((CHIPS, ROWS, COLS), F32),
+                vm((CHIPS, ROWS, COLS), BF16), vm((CHIPS, ROWS, COLS), BF16), vm((N, ROWS, COLS), BF16),
+                dma((7,)), dma((SLOTS,)), dma((SLOTS,)), dma((2, FF // MTILE)),
+                dma((EARLY, N)), dma((EARLY, N)), dma((EARLY, N)), dma((EARLY, N)),
+                dma((2,)), dma((2,)), dma((2, CHIPS, 2)), dma((2, CHIPS, 2)),
+                dma((CHIPS,)), dma((CHIPS,)), dma((PARTS, CHIPS)), dma((PARTS, CHIPS)),
+                dma((PARTS, CHIPS)), dma((PARTS, CHIPS)), dma((PARTS, CHIPS)), dma((PARTS, CHIPS)),
             ],
-            compiler_params=pltpu.CompilerParams(collective_id=0, has_side_effects=True, vmem_limit_bytes=66_000_000),
+            compiler_params=pltpu.CompilerParams(collective_id=0, has_side_effects=True, vmem_limit_bytes=58_000_000),
             name="layer",
-        )(x, k, v, gain_a.reshape(1, D), wq, wo, gain_m.reshape(1, D), w_gate, w_up, w_down, jnp.asarray(turns()))
+        )(x, k, v, gain_a.reshape(24, 128), wq, wo, gain_m.reshape(24, 128), w_gate, w_up, w_down, jnp.asarray(turns()))
 
     states, cache, columns, rows_of = P("dp", None), P("dp", None, "tp", None), P(None, "tp"), P("tp", None)
     return jax.shard_map(

time: 75.4 us -> 66.4 us (0.88)
  the two profiles are of different devices: /device:TPU:27 before, /device:TPU:0 now
where the time goes in v2:
time: 66.4 us; the launch traced here: 66.3 us
  Pallas kernels  65.5 us (99%)
  local copies, waits for them, and re-layouts  0.75 us (1%)
    pallas_call x1, Pallas kernels, step(): pl.pallas_call(kernel, out_shape=pltpu.VMEM((ROWS, D), BF16), in_specs=[p...  65.5 us

profile of v2, /device:TPU:0, one launch (start us, length us, event | category | flops | bytes accessed | tf_op | source)
XLA Modules:
  0.0 66.3 jit_solution(2581410185683645646)
XLA Ops:
  0.0 65.5 %layer.1 = bf16[64,3072]{1,0:T(8,128)(2,1)S(1)} custom-call(bf16[64,3072]{1,0:T(8,128)(2,1)} %x_h.1, bf16[16,1536,1024]{2,1,0:T(8,128)(2,1)} %bitcast.8, bf16[16,1536,1024]{2,1,0:T(8,128)(2,1)} %bitcast.9, bf16[24,128]{1,0:T(8,128)(2,1)} %bitcast.10, bf16[3072,384]{1,0:T(8,128)(2,1)} %wq_h.1, bf16[384,3072]{1,0:T(8,128)(2,1)} %wo_h.1, ...), custom_call_target="tpu_custom_call" | custom-call | tf_op jit(solution)/shard_map/layer/pallas_call | solution.py:387
  65.5 0.7 %copy.13 = bf16[64,3072]{1,0:T(8,128)(2,1)} copy(bf16[64,3072]{1,0:T(8,128)(2,1)S(1)} %layer.1) | data formatting | bytes 786432

commit v3 on v2

--- a/solution.py
+++ b/solution.py
@@ -27,8 +27,8 @@
 HALF = GROUP // 2
 PER = GROUP // SEQS
 MTILE = 256
-PARTS = 2
-PART = ROWS // PARTS
+PART = 16
+PARTS = EARLY * GROUP // PART
 F32, BF16 = jnp.float32, jnp.bfloat16
 
 
@@ -44,9 +44,9 @@
 def kernel(x_h, k_h, v_h, ga_h, wq_h, wo_h, gm_h, wg_h, wu_h, wd_h, cs_h, out_h,
            x_v, ga_v, gm_v, cs_v, wq_v, wo_v, wg_v, wu_v, wd_v, k_v, v_v,
            a_v, q_s, p_s, seen_s, term_s, tsend, trecv, psend, precv, chips, h_v, hid_v,
-           ysend, yrecv, yown, ysum, yfar, y_v,
+           ysend, yrecv, yown, ysum, yfar, y_v, zown, zsend, zrecv,
            in_sem, k_sem, v_sem, w_sem, rs_s, rs_r, ag_s, ag_r, pair_s, pair_r, chip_s, chip_r,
-           in2_s, in2_r, rs2_s, rs2_r, ag2_s, ag2_r, out2_s, out2_r):
+           in2_s, in2_r, rs2_s, rs2_r, ag2_s, ag2_r, out2_s, out2_r, rs3_s, rs3_r, ag3_s, ag3_r):
     me = lax.axis_index("tp")
 
     z, core = me // 2, lax.rem(me, 2)
@@ -148,33 +148,34 @@
     def group_rows(g):
         return pl.ds(pl.multiple_of(g * GROUP, GROUP), GROUP)
 
-    def rs_copy(g, k):
-        return remote(tsend.at[g, peer(k)], trecv.at[g, k], rs_s.at[g, k], rs_r.at[g, k], peer(k))
-
-    def ag_copy(g, k):
-        block = h_v.at[me, group_rows(g), :]
+    def rs_copy(g, k, size=GROUP):
+        part = pl.ds(0, size)
+        return remote(tsend.at[g, peer(k), part], trecv.at[g, k, part], rs_s.at[g, k], rs_r.at[g, k], peer(k))
+
+    def ag_copy(g, k, rows):
+        block = h_v.at[me, rows, :]
         return remote(block, block, ag_s.at[g, k], ag_r.at[g, k], peer(k))
 
-    def send_terms(g):
-        seen = seen_s[group_rows(g), :].astype(BF16)
-        term = dot(seen, wo_v[...])
+    FIRST, LAST = (pl.ds(EARLY * GROUP + t * HALF, HALF) for t in range(2))
+
+    def send_terms(g, rows, size):
+        term = dot(seen_s[rows, :].astype(BF16), wo_v[...])
         for j in range(N):
             block = term[:, j * COLS:(j + 1) * COLS]
-            term_s[g, j] = block
-            tsend[g, j] = block.astype(BF16)
+            term_s[g, j, :size] = block
+            tsend[g, j, :size] = block.astype(BF16)
         for k in range(1, N):
-            rs_copy(g, k).start()
-
-    def finish_h(g):
-        rows = group_rows(g)
-        total = term_s[g, me]
+            rs_copy(g, k, size).start()
+
+    def finish_h(g, rows, size):
+        total = term_s[g, me, :size]
         for k in range(1, N):
-            rs_copy(g, k).wait_recv()
-            total = total + trecv[g, k].astype(F32)
+            rs_copy(g, k, size).wait_recv()
+            total = total + trecv[g, k, :size].astype(F32)
         mine = x_v[rows, pl.ds(pl.multiple_of(me * COLS, COLS), COLS)].astype(F32)
         h_v[me, rows, :] = (mine + total).astype(BF16)
         for k in range(1, N):
-            ag_copy(g, k).start()
+            ag_copy(g, k, rows).start()
 
     def norm_h(rows):
         wide = [h_v[j, rows, :].astype(F32) for j in range(N)]
@@ -186,42 +187,38 @@
 
     def early_h(g, _):
         for k in range(1, N):
-            ag_copy(g, k).wait_recv()
+            ag_copy(g, k, group_rows(g)).wait_recv()
         norm_h(group_rows(g))
         return 0
 
-    def pair_copy(t):
-        return remote(psend.at[t], precv.at[t], pair_s.at[t], pair_r.at[t], partner)
-
-    def chip_copy(t, k, to, source):
+    pair_copy = remote(psend, precv, pair_s, pair_r, partner)
+
+    def chip_copy(k, to, source):
         part = pl.ds(source * CHIPS, CHIPS)
-        return remote(chips.at[t, 0, part], chips.at[t, k, part], chip_s.at[t, k, to], chip_r.at[t, k, source], 2 * chip(k) + to)
-
-    def late_rows(t):
-        return pl.ds(EARLY * GROUP + t * HALF, HALF)
-
-    def send_pair(t):
-        term = dot(seen_s[late_rows(t), :].astype(BF16), wo_v[...])
+        return remote(chips.at[0, part], chips.at[k, part], chip_s.at[k, to], chip_r.at[k, source], 2 * chip(k) + to)
+
+    def send_pair():
+        term = dot(seen_s[LAST, :].astype(BF16), wo_v[...])
         for j in range(N):
-            psend[t, j] = term[:, j * COLS:(j + 1) * COLS].astype(BF16)
-        pair_copy(t).start()
-
-    def send_chip(t):
-        pair_copy(t).wait_recv()
-        chips[t, 0] = (psend[t].astype(F32) + precv[t].astype(F32)).astype(BF16)
+            psend[j] = term[:, j * COLS:(j + 1) * COLS].astype(BF16)
+        pair_copy.start()
+
+    def send_chip():
+        pair_copy.wait_recv()
+        chips[0] = (psend[...].astype(F32) + precv[...].astype(F32)).astype(BF16)
         for k in (2, 1, 3):
             for to in range(2):
-                chip_copy(t, k, to, core).start()
-
-    def late_h(t):
+                chip_copy(k, to, core).start()
+
+    def last_h():
         for k in range(1, CHIPS):
             for source in range(2):
-                chip_copy(t, k, 0, source).wait_recv()
+                chip_copy(k, 0, source).wait_recv()
         for j in range(N):
-            total = x_v[late_rows(t), j * COLS:(j + 1) * COLS].astype(F32)
+            total = x_v[LAST, j * COLS:(j + 1) * COLS].astype(F32)
             for q in range(CHIPS):
-                total = total + chips[t, lax.rem(z - q + CHIPS, CHIPS), j].astype(F32)
-            h_v[j, late_rows(t), :] = total.astype(BF16)
+                total = total + chips[lax.rem(z - q + CHIPS, CHIPS), j].astype(F32)
+            h_v[j, LAST, :] = total.astype(BF16)
 
     p_s[...] = weights_of(0)
     wo_in.wait()
@@ -250,42 +247,45 @@
 
         @pl.when(lax.rem(c, PER) == 0)
         def _():
-            send_terms(c // PER - 1)
+            send_terms(c // PER - 1, group_rows(c // PER - 1), GROUP)
 
         @pl.when(c == CHUNKS - 2)
         def _():
-            send_pair(0)
-
-        @pl.when(c == CHUNKS - 1)
-        def _():
-            send_chip(0)
-
-        @pl.when(jnp.logical_and(lax.rem(c, PER) == PER - 1, c >= 2 * PER - 1))
-        def _():
-            finish_h(c // PER - 1)
+            send_terms(EARLY, FIRST, HALF)
+
+        @pl.when(jnp.logical_and(lax.rem(c, PER) == 2, c >= PER + 2))
+        def _():
+            finish_h(c // PER - 1, group_rows(c // PER - 1), GROUP)
 
         return 0
 
     lax.fori_loop(1, CHUNKS, chunk, 0)
     v_in(CHUNKS - 1).wait()
     values_of(CHUNKS - 1, p_s[...])
-    send_pair(1)
-    late_h(0)
-    send_chip(1)
+    send_pair()
+    finish_h(EARLY, FIRST, HALF)
+    send_chip()
     lax.fori_loop(0, EARLY, early_h, 0)
-    late_h(1)
-    norm_h(group_rows(EARLY))
-
-    def hidden(n, _):
+
+    ONE, TWO = pl.ds(0, EARLY * GROUP), pl.ds(EARLY * GROUP, GROUP)
+
+    def hidden(rows, n):
+        cols = pl.ds(pl.multiple_of(n * MTILE, MTILE), MTILE)
+        gate = dot(a_v[rows, :], wg_v[:, cols])
+        up = dot(a_v[rows, :], wu_v[:, cols])
+        hid_v[rows, cols] = (jax.nn.silu(gate) * up).astype(BF16)
+
+    def hidden_one(n, _):
         for w in w_in(n):
             w.wait()
-        cols = pl.ds(pl.multiple_of(n * MTILE, MTILE), MTILE)
-        gate = dot(a_v[...], wg_v[:, cols])
-        up = dot(a_v[...], wu_v[:, cols])
-        hid_v[:, cols] = (jax.nn.silu(gate) * up).astype(BF16)
-        return 0
-
-    lax.fori_loop(0, FF // MTILE, hidden, 0)
+        hidden(ONE, n)
+        return 0
+
+    def hidden_two(n, _):
+        hidden(TWO, n)
+        return 0
+
+    lax.fori_loop(0, FF // MTILE, hidden_one, 0)
     wd_in.wait()
 
     def in2(q):
@@ -308,7 +308,14 @@
         return remote(b, b, out2_s.at[r, k], out2_r.at[r, k], partner)
 
     def down(half):
-        return dot(hid_v[...], wd_v[:, pl.ds(pl.multiple_of(half * CHIPS * COLS, CHIPS * COLS), CHIPS * COLS)])
+        return dot(hid_v[ONE, :], wd_v[:, pl.ds(pl.multiple_of(half * CHIPS * COLS, CHIPS * COLS), CHIPS * COLS)])
+
+    def rs3(k):
+        return remote(zsend.at[peer(k)], zrecv.at[k], rs3_s.at[k], rs3_r.at[k], peer(k))
+
+    def ag3(k):
+        b = y_v.at[me, TWO]
+        return remote(b, b, ag3_s.at[k], ag3_r.at[k], peer(k))
 
     theirs = down(1 - core)
     for q in range(CHIPS):
@@ -322,11 +329,24 @@
         q = chip(k)
         in2(q).wait_recv()
         ysum[q] = (yown[q] + yrecv[q].astype(F32)).astype(BF16)
-        rs2(0, k).start()
-    for r in range(1, PARTS):
+    for r in range(PARTS):
         for k in (2, 1, 3):
             rs2(r, k).start()
     in2(z).wait_recv()
+
+    for k in range(1, N):
+        ag_copy(EARLY, k, FIRST).wait_recv()
+    last_h()
+    norm_h(TWO)
+    lax.fori_loop(0, FF // MTILE, hidden_two, 0)
+    last = dot(hid_v[TWO, :], wd_v[...])
+    for j in range(N):
+        block = last[:, j * COLS:(j + 1) * COLS]
+        zown[j] = block
+        zsend[j] = block.astype(BF16)
+    for k in range(1, N):
+        rs3(k).start()
+
     for r in range(PARTS):
         rows = part_rows(r)
         total = yown[z, rows, :] + yrecv[z, rows, :].astype(F32)
@@ -336,6 +356,13 @@
         y_v[mine, rows, :] = (h_v[mine, rows, :].astype(F32) + total).astype(BF16)
         for k in (2, 1, 3, 0):
             ag2(r, k, mine).start()
+    total = zown[me]
+    for k in range(1, N):
+        rs3(k).wait_recv()
+        total = total + zrecv[k].astype(F32)
+    y_v[me, TWO, :] = (h_v[me, TWO, :].astype(F32) + total).astype(BF16)
+    for k in range(1, N):
+        ag3(k).start()
     for r in range(PARTS):
         for k in (1, 3, 2):
             block = core * CHIPS + chip(CHIPS - k)
@@ -345,21 +372,27 @@
         ag2(r, 0, mine).wait_recv()
         for k in range(1, CHIPS):
             out2(r, k, mine).wait_recv()
+    for k in range(1, N):
+        ag3(k).wait_recv()
     for j in range(N):
         out_h[:, j * COLS:(j + 1) * COLS] = y_v[j]
 
     def sent(g, _):
         for k in range(1, N):
             rs_copy(g, k).wait_send()
-            ag_copy(g, k).wait_send()
+            ag_copy(g, k, group_rows(g)).wait_send()
         return 0
 
     lax.fori_loop(0, EARLY, sent, 0)
-    for t in range(2):
-        pair_copy(t).wait_send()
-        for k in range(1, CHIPS):
-            for to in range(2):
-                chip_copy(t, k, to, core).wait_send()
+    for k in range(1, N):
+        rs_copy(EARLY, k, HALF).wait_send()
+        ag_copy(EARLY, k, FIRST).wait_send()
+        rs3(k).wait_send()
+        ag3(k).wait_send()
+    pair_copy.wait_send()
+    for k in range(1, CHIPS):
+        for to in range(2):
+            chip_copy(k, to, core).wait_send()
     for q in range(CHIPS):
         in2(q).wait_send()
     for r in range(PARTS):
@@ -394,16 +427,18 @@
                 vm((D, QD), BF16), vm((QD, D), BF16), vm((D, FF), BF16), vm((D, FF), BF16), vm((FF, D), BF16),
                 vm((SLOTS, SEQS * QD, CACHE), BF16), vm((SLOTS, SEQS * QD, CACHE), BF16),
                 vm((ROWS, D), BF16), vm((ROWS, QD), F32), vm((SEQS * HEADS, CACHE), BF16), vm((ROWS, QD), F32),
-                vm((EARLY, N, GROUP, COLS), F32), vm((EARLY, N, GROUP, COLS), BF16), vm((EARLY, N, GROUP, COLS), BF16),
-                vm((2, N, HALF, COLS), BF16), vm((2, N, HALF, COLS), BF16), vm((2, CHIPS, N, HALF, COLS), BF16),
+                vm((GROUPS, N, GROUP, COLS), F32), vm((GROUPS, N, GROUP, COLS), BF16), vm((GROUPS, N, GROUP, COLS), BF16),
+                vm((N, HALF, COLS), BF16), vm((N, HALF, COLS), BF16), vm((CHIPS, N, HALF, COLS), BF16),
                 vm((N, ROWS, COLS), BF16), vm((ROWS, FF), BF16),
-                vm((CHIPS, ROWS, COLS), BF16), vm((CHIPS, ROWS, COLS), BF16), vm((CHIPS, ROWS, COLS), F32),
-                vm((CHIPS, ROWS, COLS), BF16), vm((CHIPS, ROWS, COLS), BF16), vm((N, ROWS, COLS), BF16),
+                vm((CHIPS, EARLY * GROUP, COLS), BF16), vm((CHIPS, EARLY * GROUP, COLS), BF16), vm((CHIPS, EARLY * GROUP, COLS), F32),
+                vm((CHIPS, EARLY * GROUP, COLS), BF16), vm((CHIPS, EARLY * GROUP, COLS), BF16), vm((N, ROWS, COLS), BF16),
+                vm((N, GROUP, COLS), F32), vm((N, GROUP, COLS), BF16), vm((N, GROUP, COLS), BF16),
                 dma((7,)), dma((SLOTS,)), dma((SLOTS,)), dma((2, FF // MTILE)),
-                dma((EARLY, N)), dma((EARLY, N)), dma((EARLY, N)), dma((EARLY, N)),
-                dma((2,)), dma((2,)), dma((2, CHIPS, 2)), dma((2, CHIPS, 2)),
+                dma((GROUPS, N)), dma((GROUPS, N)), dma((GROUPS, N)), dma((GROUPS, N)),
+                dma, dma, dma((CHIPS, 2)), dma((CHIPS, 2)),
                 dma((CHIPS,)), dma((CHIPS,)), dma((PARTS, CHIPS)), dma((PARTS, CHIPS)),
                 dma((PARTS, CHIPS)), dma((PARTS, CHIPS)), dma((PARTS, CHIPS)), dma((PARTS, CHIPS)),
+                dma((N,)), dma((N,)), dma((N,)), dma((N,)),
             ],
             compiler_params=pltpu.CompilerParams(collective_id=0, has_side_effects=True, vmem_limit_bytes=58_000_000),
             name="layer",

time: 66.4 us -> 63 us (0.949)
  Pallas kernels: 65.5 us -> 62.1 us
    pallas_call x1, Pallas kernels: 65.5 us -> 62.1 us  [step(): pl.pallas_call(kernel, out_shape=pltpu.VMEM((ROWS, D), BF16), in_specs=[p...]
where the time goes in v3:
time: 63 us; the launch traced here: 62.8 us
  Pallas kernels  62.1 us (99%)
  local copies, waits for them, and re-layouts  0.75 us (1%)
    pallas_call x1, Pallas kernels, step(): pl.pallas_call(kernel, out_shape=pltpu.VMEM((ROWS, D), BF16), in_specs=[p...  62.1 us

profile of v3, /device:TPU:0, one launch (start us, length us, event | category | flops | bytes accessed | tf_op | source)
XLA Modules:
  0.0 62.8 jit_solution(14526312618659749456)
XLA Ops:
  0.0 62.1 %layer.1 = bf16[64,3072]{1,0:T(8,128)(2,1)S(1)} custom-call(bf16[64,3072]{1,0:T(8,128)(2,1)} %x_h.1, bf16[16,1536,1024]{2,1,0:T(8,128)(2,1)} %bitcast.8, bf16[16,1536,1024]{2,1,0:T(8,128)(2,1)} %bitcast.9, bf16[24,128]{1,0:T(8,128)(2,1)} %bitcast.10, bf16[3072,384]{1,0:T(8,128)(2,1)} %wq_h.1, bf16[384,3072]{1,0:T(8,128)(2,1)} %wo_h.1, ...), custom_call_target="tpu_custom_call" | custom-call | tf_op jit(solution)/shard_map/layer/pallas_call | solution.py:420
  62.1 0.7 %copy.13 = bf16[64,3072]{1,0:T(8,128)(2,1)} copy(bf16[64,3072]{1,0:T(8,128)(2,1)S(1)} %layer.1) | data formatting | bytes 786432

commit v4 on v3

--- a/solution.py
+++ b/solution.py
@@ -46,7 +46,7 @@
            a_v, q_s, p_s, seen_s, term_s, tsend, trecv, psend, precv, chips, h_v, hid_v,
            ysend, yrecv, yown, ysum, yfar, y_v, zown, zsend, zrecv,
            in_sem, k_sem, v_sem, w_sem, rs_s, rs_r, ag_s, ag_r, pair_s, pair_r, chip_s, chip_r,
-           in2_s, in2_r, rs2_s, rs2_r, ag2_s, ag2_r, out2_s, out2_r, rs3_s, rs3_r, ag3_s, ag3_r):
+           in2_s, in2_r, rs2_s, rs2_r, ag2_r, out2_s, out2_r, rs3_s, rs3_r, ag3_s, ag3_r):
     me = lax.axis_index("tp")
 
     z, core = me // 2, lax.rem(me, 2)
@@ -57,6 +57,9 @@
 
     def chip(k):
         return lax.rem(z + k, CHIPS)
+
+    def arrived(like, sem):
+        pltpu.make_async_copy(like, like, sem).wait()
 
     def remote(src, dst, send_sem, recv_sem, target):
         return pltpu.make_async_remote_copy(
@@ -81,12 +84,9 @@
         s = lax.rem(c, SLOTS)
         return local(v_h.at[c], v_v.at[s], v_sem.at[s])
 
-    def w_in(n):
-        cols = pl.ds(n * MTILE, MTILE)
-        return (local(wg_h.at[:, cols], wg_v.at[:, cols], w_sem.at[0, n]),
-                local(wu_h.at[:, cols], wu_v.at[:, cols], w_sem.at[1, n]))
-
-    wd_in = local(wd_h, wd_v, in_sem.at[6])
+    wg_in = local(wg_h, wg_v, w_sem.at[0])
+    wu_in = local(wu_h, wu_v, w_sem.at[1])
+    wd_in = local(wd_h, wd_v, w_sem.at[2])
 
     x_in.start()
     ga_in.start()
@@ -102,7 +102,6 @@
     barrier = pltpu.get_barrier_semaphore()
     for k in range(1, N):
         pl.semaphore_signal(barrier, inc=1, device_id={"tp": peer(k)}, device_id_type=pl.DeviceIdType.MESH)
-    pl.semaphore_wait(barrier, N - 1)
 
     x_in.wait()
     ga_in.wait()
@@ -150,11 +149,11 @@
 
     def rs_copy(g, k, size=GROUP):
         part = pl.ds(0, size)
-        return remote(tsend.at[g, peer(k), part], trecv.at[g, k, part], rs_s.at[g, k], rs_r.at[g, k], peer(k))
+        return remote(tsend.at[g, peer(k), part], trecv.at[g, k, part], rs_s.at[g], rs_r.at[g], peer(k))
 
     def ag_copy(g, k, rows):
         block = h_v.at[me, rows, :]
-        return remote(block, block, ag_s.at[g, k], ag_r.at[g, k], peer(k))
+        return remote(block, block, ag_s.at[g], ag_r.at[g], peer(k))
 
     FIRST, LAST = (pl.ds(EARLY * GROUP + t * HALF, HALF) for t in range(2))
 
@@ -168,9 +167,9 @@
             rs_copy(g, k, size).start()
 
     def finish_h(g, rows, size):
+        arrived(trecv.at[g, pl.ds(1, N - 1), pl.ds(0, size)], rs_r.at[g])
         total = term_s[g, me, :size]
         for k in range(1, N):
-            rs_copy(g, k, size).wait_recv()
             total = total + trecv[g, k, :size].astype(F32)
         mine = x_v[rows, pl.ds(pl.multiple_of(me * COLS, COLS), COLS)].astype(F32)
         h_v[me, rows, :] = (mine + total).astype(BF16)
@@ -186,16 +185,15 @@
             a_v[rows, cols] = (wide[j] * scale * gain_of(gm_v, j * COLS, COLS)).astype(BF16)
 
     def early_h(g, _):
-        for k in range(1, N):
-            ag_copy(g, k, group_rows(g)).wait_recv()
+        arrived(h_v.at[pl.ds(0, N - 1), group_rows(g)], ag_r.at[g])
         norm_h(group_rows(g))
         return 0
 
     pair_copy = remote(psend, precv, pair_s, pair_r, partner)
 
-    def chip_copy(k, to, source):
-        part = pl.ds(source * CHIPS, CHIPS)
-        return remote(chips.at[0, part], chips.at[k, part], chip_s.at[k, to], chip_r.at[k, source], 2 * chip(k) + to)
+    def chip_copy(k, to):
+        part = pl.ds(core * CHIPS, CHIPS)
+        return remote(chips.at[0, part], chips.at[k, part], chip_s, chip_r, 2 * chip(k) + to)
 
     def send_pair():
         term = dot(seen_s[LAST, :].astype(BF16), wo_v[...])
@@ -208,12 +206,10 @@
         chips[0] = (psend[...].astype(F32) + precv[...].astype(F32)).astype(BF16)
         for k in (2, 1, 3):
             for to in range(2):
-                chip_copy(k, to, core).start()
+                chip_copy(k, to).start()
 
     def last_h():
-        for k in range(1, CHIPS):
-            for source in range(2):
-                chip_copy(k, 0, source).wait_recv()
+        arrived(chips.at[pl.ds(1, CHIPS - 1)], chip_r)
         for j in range(N):
             total = x_v[LAST, j * COLS:(j + 1) * COLS].astype(F32)
             for q in range(CHIPS):
@@ -221,9 +217,6 @@
             h_v[j, LAST, :] = total.astype(BF16)
 
     p_s[...] = weights_of(0)
-    wo_in.wait()
-    gm_in.wait()
-
     def chunk(c, _):
         @pl.when(c + SLOTS - 1 < CHUNKS)
         def _():
@@ -235,15 +228,19 @@
 
         @pl.when(c == CHUNKS - SLOTS + 1)
         def _():
-            for n in range(FF // MTILE):
-                for w in w_in(n):
-                    w.start()
-            wd_in.start()
+            for w in (wg_in, wu_in, wd_in):
+                w.start(priority=1)
 
         v_in(c - 1).wait()
         p = p_s[...]
         p_s[...] = weights_of(c)
         values_of(c - 1, p)
+
+        @pl.when(c == PER)
+        def _():
+            pl.semaphore_wait(barrier, N - 1)
+            wo_in.wait()
+            gm_in.wait()
 
         @pl.when(lax.rem(c, PER) == 0)
         def _():
@@ -275,70 +272,60 @@
         up = dot(a_v[rows, :], wu_v[:, cols])
         hid_v[rows, cols] = (jax.nn.silu(gate) * up).astype(BF16)
 
-    def hidden_one(n, _):
-        for w in w_in(n):
-            w.wait()
+    wg_in.wait()
+    wu_in.wait()
+    for n in range(FF // MTILE):
         hidden(ONE, n)
-        return 0
-
-    def hidden_two(n, _):
-        hidden(TWO, n)
-        return 0
-
-    lax.fori_loop(0, FF // MTILE, hidden_one, 0)
     wd_in.wait()
 
-    def in2(q):
-        return remote(ysend.at[q], yrecv.at[q], in2_s.at[q], in2_r.at[q], partner)
+    in2 = remote(ysend, yrecv, in2_s, in2_r, partner)
 
     def part_rows(r):
         return pl.ds(r * PART, PART)
 
     def rs2(r, k):
-        return remote(ysum.at[chip(k), part_rows(r)], yfar.at[k, part_rows(r)], rs2_s.at[r, k], rs2_r.at[r, k], 2 * chip(k) + core)
+        return remote(ysum.at[chip(k), part_rows(r)], yfar.at[k, part_rows(r)], rs2_s, rs2_r.at[r], 2 * chip(k) + core)
 
     mine = core * CHIPS + z
 
-    def ag2(r, k, block):
-        b = y_v.at[block, part_rows(r)]
-        return remote(b, b, ag2_s.at[r, k], ag2_r.at[r, k], partner if k == 0 else 2 * chip(k) + core)
-
-    def out2(r, k, block):
-        b = y_v.at[block, part_rows(r)]
-        return remote(b, b, out2_s.at[r, k], out2_r.at[r, k], partner)
+    def ag2(r, k):
+        b = y_v.at[mine, part_rows(r)]
+        return remote(b, b, out2_s, ag2_r.at[r], 2 * chip(k) + core)
+
+    def out2(r, k):
+        b = y_v.at[core * CHIPS + chip(CHIPS - k), part_rows(r)]
+        return remote(b, b, out2_s, out2_r, partner)
 
     def down(half):
         return dot(hid_v[ONE, :], wd_v[:, pl.ds(pl.multiple_of(half * CHIPS * COLS, CHIPS * COLS), CHIPS * COLS)])
 
     def rs3(k):
-        return remote(zsend.at[peer(k)], zrecv.at[k], rs3_s.at[k], rs3_r.at[k], peer(k))
+        return remote(zsend.at[peer(k)], zrecv.at[k], rs3_s, rs3_r, peer(k))
 
     def ag3(k):
         b = y_v.at[me, TWO]
-        return remote(b, b, ag3_s.at[k], ag3_r.at[k], peer(k))
+        return remote(b, b, ag3_s, ag3_r, peer(k))
 
     theirs = down(1 - core)
     for q in range(CHIPS):
         ysend[q] = theirs[:, q * COLS:(q + 1) * COLS].astype(BF16)
-    for k in (2, 1, 3, 0):
-        in2(chip(k)).start()
+    in2.start()
     ours = down(core)
     for q in range(CHIPS):
         yown[q] = ours[:, q * COLS:(q + 1) * COLS]
+    in2.wait_recv()
     for k in (2, 1, 3):
         q = chip(k)
-        in2(q).wait_recv()
         ysum[q] = (yown[q] + yrecv[q].astype(F32)).astype(BF16)
     for r in range(PARTS):
         for k in (2, 1, 3):
             rs2(r, k).start()
-    in2(z).wait_recv()
-
-    for k in range(1, N):
-        ag_copy(EARLY, k, FIRST).wait_recv()
+
+    arrived(h_v.at[pl.ds(0, N - 1), FIRST], ag_r.at[EARLY])
     last_h()
     norm_h(TWO)
-    lax.fori_loop(0, FF // MTILE, hidden_two, 0)
+    for n in range(FF // MTILE):
+        hidden(TWO, n)
     last = dot(hid_v[TWO, :], wd_v[...])
     for j in range(N):
         block = last[:, j * COLS:(j + 1) * COLS]
@@ -350,57 +337,40 @@
     for r in range(PARTS):
         rows = part_rows(r)
         total = yown[z, rows, :] + yrecv[z, rows, :].astype(F32)
+        arrived(yfar.at[pl.ds(1, CHIPS - 1), rows], rs2_r.at[r])
         for k in range(1, CHIPS):
-            rs2(r, k).wait_recv()
             total = total + yfar[k, rows, :].astype(F32)
         y_v[mine, rows, :] = (h_v[mine, rows, :].astype(F32) + total).astype(BF16)
-        for k in (2, 1, 3, 0):
-            ag2(r, k, mine).start()
+        for k in (2, 1, 3):
+            ag2(r, k).start()
+        out2(r, 0).start()
+    arrived(zrecv.at[pl.ds(1, N - 1)], rs3_r)
     total = zown[me]
     for k in range(1, N):
-        rs3(k).wait_recv()
         total = total + zrecv[k].astype(F32)
     y_v[me, TWO, :] = (h_v[me, TWO, :].astype(F32) + total).astype(BF16)
     for k in range(1, N):
         ag3(k).start()
     for r in range(PARTS):
+        arrived(y_v.at[pl.ds(0, CHIPS - 1), part_rows(r)], ag2_r.at[r])
         for k in (1, 3, 2):
-            block = core * CHIPS + chip(CHIPS - k)
-            ag2(r, k, block).wait_recv()
-            out2(r, k, block).start()
-    for r in range(PARTS):
-        ag2(r, 0, mine).wait_recv()
-        for k in range(1, CHIPS):
-            out2(r, k, mine).wait_recv()
-    for k in range(1, N):
-        ag3(k).wait_recv()
+            out2(r, k).start()
+    arrived(y_v.at[pl.ds(0, CHIPS), ONE], out2_r)
+    arrived(y_v.at[pl.ds(0, N - 1), TWO], ag3_r)
     for j in range(N):
         out_h[:, j * COLS:(j + 1) * COLS] = y_v[j]
 
-    def sent(g, _):
-        for k in range(1, N):
-            rs_copy(g, k).wait_send()
-            ag_copy(g, k, group_rows(g)).wait_send()
-        return 0
-
-    lax.fori_loop(0, EARLY, sent, 0)
-    for k in range(1, N):
-        rs_copy(EARLY, k, HALF).wait_send()
-        ag_copy(EARLY, k, FIRST).wait_send()
-        rs3(k).wait_send()
-        ag3(k).wait_send()
+    for g in range(GROUPS):
+        part = pl.ds(0, GROUP if g < EARLY else HALF)
+        arrived(tsend.at[g, pl.ds(0, N - 1), part], rs_s.at[g])
+        arrived(tsend.at[g, pl.ds(0, N - 1), part], ag_s.at[g])
     pair_copy.wait_send()
-    for k in range(1, CHIPS):
-        for to in range(2):
-            chip_copy(k, to, core).wait_send()
-    for q in range(CHIPS):
-        in2(q).wait_send()
-    for r in range(PARTS):
-        ag2(r, 0, mine).wait_send()
-        for k in range(1, CHIPS):
-            rs2(r, k).wait_send()
-            ag2(r, k, mine).wait_send()
-            out2(r, k, mine).wait_send()
+    arrived(chips.at[pl.ds(0, CHIPS - 1)], chip_s)
+    in2.wait_send()
+    arrived(ysum.at[pl.ds(0, CHIPS - 1)], rs2_s)
+    arrived(y_v.at[pl.ds(0, N - 1), ONE], out2_s)
+    arrived(zsend.at[pl.ds(0, N - 1)], rs3_s)
+    arrived(zsend.at[pl.ds(0, N - 1)], ag3_s)
 
 
 def turns():
@@ -433,12 +403,10 @@
                 vm((CHIPS, EARLY * GROUP, COLS), BF16), vm((CHIPS, EARLY * GROUP, COLS), BF16), vm((CHIPS, EARLY * GROUP, COLS), F32),
                 vm((CHIPS, EARLY * GROUP, COLS), BF16), vm((CHIPS, EARLY * GROUP, COLS), BF16), vm((N, ROWS, COLS), BF16),
                 vm((N, GROUP, COLS), F32), vm((N, GROUP, COLS), BF16), vm((N, GROUP, COLS), BF16),
-                dma((7,)), dma((SLOTS,)), dma((SLOTS,)), dma((2, FF // MTILE)),
-                dma((GROUPS, N)), dma((GROUPS, N)), dma((GROUPS, N)), dma((GROUPS, N)),
-                dma, dma, dma((CHIPS, 2)), dma((CHIPS, 2)),
-                dma((CHIPS,)), dma((CHIPS,)), dma((PARTS, CHIPS)), dma((PARTS, CHIPS)),
-                dma((PARTS, CHIPS)), dma((PARTS, CHIPS)), dma((PARTS, CHIPS)), dma((PARTS, CHIPS)),
-                dma((N,)), dma((N,)), dma((N,)), dma((N,)),
+                dma((6,)), dma((SLOTS,)), dma((SLOTS,)), dma((3,)),
+                dma((GROUPS,)), dma((GROUPS,)), dma((GROUPS,)), dma((GROUPS,)),
+                dma, dma, dma, dma,
+                dma, dma, dma, dma((PARTS,)), dma((PARTS,)), dma, dma, dma, dma, dma, dma,
             ],
             compiler_params=pltpu.CompilerParams(collective_id=0, has_side_effects=True, vmem_limit_bytes=58_000_000),
             name="layer",

time: 63 us -> 57.9 us (0.919)
  Pallas kernels: 62.1 us -> 57 us
    pallas_call x1, Pallas kernels: 62.1 us -> 57 us  [step(): pl.pallas_call(kernel, out_shape=pltpu.VMEM((ROWS, D), BF16), in_specs=[p...]
where the time goes in v4:
time: 57.9 us; the launch traced here: 57.8 us
  Pallas kernels  57 us (98%)
  local copies, waits for them, and re-layouts  0.75 us (1%)
    pallas_call x1, Pallas kernels, step(): pl.pallas_call(kernel, out_shape=pltpu.VMEM((ROWS, D), BF16), in_specs=[p...  57 us

profile of v4, /device:TPU:0, one launch (start us, length us, event | category | flops | bytes accessed | tf_op | source)
XLA Modules:
  0.0 57.8 jit_solution(6771310075440730957)
XLA Ops:
  0.0 57.0 %layer.1 = bf16[64,3072]{1,0:T(8,128)(2,1)S(1)} custom-call(bf16[64,3072]{1,0:T(8,128)(2,1)} %x_h.1, bf16[16,1536,1024]{2,1,0:T(8,128)(2,1)} %bitcast.8, bf16[16,1536,1024]{2,1,0:T(8,128)(2,1)} %bitcast.9, bf16[24,128]{1,0:T(8,128)(2,1)} %bitcast.10, bf16[3072,384]{1,0:T(8,128)(2,1)} %wq_h.1, bf16[384,3072]{1,0:T(8,128)(2,1)} %wo_h.1, ...), custom_call_target="tpu_custom_call" | custom-call | tf_op jit(solution)/shard_map/layer/pallas_call | solution.py:390
  57.1 0.7 %copy.13 = bf16[64,3072]{1,0:T(8,128)(2,1)} copy(bf16[64,3072]{1,0:T(8,128)(2,1)S(1)} %layer.1) | data formatting | bytes 786432

commit v5 on v4

--- a/solution.py
+++ b/solution.py
@@ -45,8 +45,8 @@
            x_v, ga_v, gm_v, cs_v, wq_v, wo_v, wg_v, wu_v, wd_v, k_v, v_v,
            a_v, q_s, p_s, seen_s, term_s, tsend, trecv, psend, precv, chips, h_v, hid_v,
            ysend, yrecv, yown, ysum, yfar, y_v, zown, zsend, zrecv,
-           in_sem, k_sem, v_sem, w_sem, rs_s, rs_r, ag_s, ag_r, pair_s, pair_r, chip_s, chip_r,
-           in2_s, in2_r, rs2_s, rs2_r, ag2_r, out2_s, out2_r, rs3_s, rs3_r, ag3_s, ag3_r):
+           in_sem, k_sem, v_sem, w_sem, rs_s, rs_r, ag_s, ag_r, pair_s, pair_r, chip_s, chip_r, forward_s, forward_r,
+           in2_s, in2_r, rs2_s, rs2_r, ag2_r, out2_s, out2_r, rs3_s, rs3_r, ag3_s, ag3_r, out3_r):
     me = lax.axis_index("tp")
 
     z, core = me // 2, lax.rem(me, 2)
@@ -57,6 +57,11 @@
 
     def chip(k):
         return lax.rem(z + k, CHIPS)
+
+    side = z // 2
+    edge = z + side * (3 - 2 * z)
+    others = [t + side * (3 - 2 * t) for t in (3, 2, 1 - edge)]
+    devices = [2 * t + c for t in others for c in (core, 1 - core)] + [partner]
 
     def arrived(like, sem):
         pltpu.make_async_copy(like, like, sem).wait()
@@ -147,13 +152,13 @@
     def group_rows(g):
         return pl.ds(pl.multiple_of(g * GROUP, GROUP), GROUP)
 
-    def rs_copy(g, k, size=GROUP):
+    def rs_copy(g, to, size):
         part = pl.ds(0, size)
-        return remote(tsend.at[g, peer(k), part], trecv.at[g, k, part], rs_s.at[g], rs_r.at[g], peer(k))
-
-    def ag_copy(g, k, rows):
+        return remote(tsend.at[g, to, part], trecv.at[g, me, part], rs_s.at[g], rs_r.at[g], to)
+
+    def ag_copy(g, to, rows):
         block = h_v.at[me, rows, :]
-        return remote(block, block, ag_s.at[g], ag_r.at[g], peer(k))
+        return remote(block, block, ag_s.at[g], ag_r.at[g], to)
 
     FIRST, LAST = (pl.ds(EARLY * GROUP + t * HALF, HALF) for t in range(2))
 
@@ -163,18 +168,18 @@
             block = term[:, j * COLS:(j + 1) * COLS]
             term_s[g, j, :size] = block
             tsend[g, j, :size] = block.astype(BF16)
-        for k in range(1, N):
-            rs_copy(g, k, size).start()
+        for to in devices:
+            rs_copy(g, to, size).start()
 
     def finish_h(g, rows, size):
         arrived(trecv.at[g, pl.ds(1, N - 1), pl.ds(0, size)], rs_r.at[g])
         total = term_s[g, me, :size]
         for k in range(1, N):
-            total = total + trecv[g, k, :size].astype(F32)
+            total = total + trecv[g, peer(k), :size].astype(F32)
         mine = x_v[rows, pl.ds(pl.multiple_of(me * COLS, COLS), COLS)].astype(F32)
         h_v[me, rows, :] = (mine + total).astype(BF16)
-        for k in range(1, N):
-            ag_copy(g, k, rows).start()
+        for to in devices:
+            ag_copy(g, to, rows).start()
 
     def norm_h(rows):
         wide = [h_v[j, rows, :].astype(F32) for j in range(N)]
@@ -191,9 +196,13 @@
 
     pair_copy = remote(psend, precv, pair_s, pair_r, partner)
 
-    def chip_copy(k, to):
-        part = pl.ds(core * CHIPS, CHIPS)
-        return remote(chips.at[0, part], chips.at[k, part], chip_s, chip_r, 2 * chip(k) + to)
+    half = pl.ds(core * CHIPS, CHIPS)
+
+    def chip_copy(to):
+        return remote(chips.at[z, half], chips.at[z, half], chip_s, chip_r, 2 * to + core)
+
+    def forward_copy(source):
+        return remote(chips.at[source, half], chips.at[source, half], forward_s, forward_r, partner)
 
     def send_pair():
         term = dot(seen_s[LAST, :].astype(BF16), wo_v[...])
@@ -203,17 +212,21 @@
 
     def send_chip():
         pair_copy.wait_recv()
-        chips[0] = (psend[...].astype(F32) + precv[...].astype(F32)).astype(BF16)
-        for k in (2, 1, 3):
-            for to in range(2):
-                chip_copy(k, to).start()
+        chips[z] = (psend[...].astype(F32) + precv[...].astype(F32)).astype(BF16)
+        for to in others:
+            chip_copy(to).start()
+
+    def forward_chips():
+        arrived(chips.at[pl.ds(0, CHIPS - 1), half], chip_r)
+        for source in others:
+            forward_copy(source).start()
 
     def last_h():
-        arrived(chips.at[pl.ds(1, CHIPS - 1)], chip_r)
+        arrived(chips.at[pl.ds(0, CHIPS - 1), half], forward_r)
         for j in range(N):
             total = x_v[LAST, j * COLS:(j + 1) * COLS].astype(F32)
             for q in range(CHIPS):
-                total = total + chips[lax.rem(z - q + CHIPS, CHIPS), j].astype(F32)
+                total = total + chips[q, j].astype(F32)
             h_v[j, LAST, :] = total.astype(BF16)
 
     p_s[...] = weights_of(0)
@@ -250,7 +263,7 @@
         def _():
             send_terms(EARLY, FIRST, HALF)
 
-        @pl.when(jnp.logical_and(lax.rem(c, PER) == 2, c >= PER + 2))
+        @pl.when(jnp.logical_or(c == CHUNKS - 2, jnp.logical_and(lax.rem(c, PER) == PER - 1, jnp.logical_and(c > PER, c < CHUNKS - 1))))
         def _():
             finish_h(c // PER - 1, group_rows(c // PER - 1), GROUP)
 
@@ -261,8 +274,9 @@
     values_of(CHUNKS - 1, p_s[...])
     send_pair()
     finish_h(EARLY, FIRST, HALF)
+    lax.fori_loop(0, EARLY - 1, early_h, 0)
     send_chip()
-    lax.fori_loop(0, EARLY, early_h, 0)
+    early_h(EARLY - 1, 0)
 
     ONE, TWO = pl.ds(0, EARLY * GROUP), pl.ds(EARLY * GROUP, GROUP)
 
@@ -283,28 +297,39 @@
     def part_rows(r):
         return pl.ds(r * PART, PART)
 
-    def rs2(r, k):
-        return remote(ysum.at[chip(k), part_rows(r)], yfar.at[k, part_rows(r)], rs2_s, rs2_r.at[r], 2 * chip(k) + core)
+    def rs2(r, to):
+        return remote(ysum.at[to, part_rows(r)], yfar.at[z, part_rows(r)], rs2_s, rs2_r.at[r], 2 * to + core)
 
     mine = core * CHIPS + z
 
-    def ag2(r, k):
+    def ag2(r, to):
         b = y_v.at[mine, part_rows(r)]
-        return remote(b, b, out2_s, ag2_r.at[r], 2 * chip(k) + core)
-
-    def out2(r, k):
-        b = y_v.at[core * CHIPS + chip(CHIPS - k), part_rows(r)]
+        return remote(b, b, out2_s, ag2_r.at[r], 2 * to + core)
+
+    def out2(r, source):
+        b = y_v.at[core * CHIPS + source, part_rows(r)]
         return remote(b, b, out2_s, out2_r, partner)
 
-    def down(half):
-        return dot(hid_v[ONE, :], wd_v[:, pl.ds(pl.multiple_of(half * CHIPS * COLS, CHIPS * COLS), CHIPS * COLS)])
-
-    def rs3(k):
-        return remote(zsend.at[peer(k)], zrecv.at[k], rs3_s, rs3_r, peer(k))
-
-    def ag3(k):
+    def down(side_of):
+        return dot(hid_v[ONE, :], wd_v[:, pl.ds(pl.multiple_of(side_of * CHIPS * COLS, CHIPS * COLS), CHIPS * COLS)])
+
+    def rs3(to):
+        return remote(zsend.at[to], zrecv.at[me], rs3_s, rs3_r, to)
+
+    def ag3(to):
         b = y_v.at[me, TWO]
-        return remote(b, b, ag3_s, ag3_r, peer(k))
+        return remote(b, b, ag3_s, ag3_r, to)
+
+    def finish_part(r):
+        rows = part_rows(r)
+        total = yown[z, rows, :] + yrecv[z, rows, :].astype(F32)
+        arrived(yfar.at[pl.ds(1, CHIPS - 1), rows], rs2_r.at[r])
+        for k in range(1, CHIPS):
+            total = total + yfar[chip(k), rows, :].astype(F32)
+        y_v[mine, rows, :] = (h_v[mine, rows, :].astype(F32) + total).astype(BF16)
+        for to in others:
+            ag2(r, to).start()
+        out2(r, z).start()
 
     theirs = down(1 - core)
     for q in range(CHIPS):
@@ -314,12 +339,12 @@
     for q in range(CHIPS):
         yown[q] = ours[:, q * COLS:(q + 1) * COLS]
     in2.wait_recv()
-    for k in (2, 1, 3):
-        q = chip(k)
+    for q in others:
         ysum[q] = (yown[q] + yrecv[q].astype(F32)).astype(BF16)
     for r in range(PARTS):
-        for k in (2, 1, 3):
-            rs2(r, k).start()
+        for to in others:
+            rs2(r, to).start()
+    forward_chips()
 
     arrived(h_v.at[pl.ds(0, N - 1), FIRST], ag_r.at[EARLY])
     last_h()
@@ -331,30 +356,22 @@
         block = last[:, j * COLS:(j + 1) * COLS]
         zown[j] = block
         zsend[j] = block.astype(BF16)
-    for k in range(1, N):
-        rs3(k).start()
+    for to in devices:
+        rs3(to).start()
 
     for r in range(PARTS):
-        rows = part_rows(r)
-        total = yown[z, rows, :] + yrecv[z, rows, :].astype(F32)
-        arrived(yfar.at[pl.ds(1, CHIPS - 1), rows], rs2_r.at[r])
-        for k in range(1, CHIPS):
-            total = total + yfar[k, rows, :].astype(F32)
-        y_v[mine, rows, :] = (h_v[mine, rows, :].astype(F32) + total).astype(BF16)
-        for k in (2, 1, 3):
-            ag2(r, k).start()
-        out2(r, 0).start()
+        finish_part(r)
     arrived(zrecv.at[pl.ds(1, N - 1)], rs3_r)
     total = zown[me]
     for k in range(1, N):
-        total = total + zrecv[k].astype(F32)
+        total = total + zrecv[peer(k)].astype(F32)
     y_v[me, TWO, :] = (h_v[me, TWO, :].astype(F32) + total).astype(BF16)
-    for k in range(1, N):
-        ag3(k).start()
+    for to in devices:
+        ag3(to).start()
     for r in range(PARTS):
         arrived(y_v.at[pl.ds(0, CHIPS - 1), part_rows(r)], ag2_r.at[r])
-        for k in (1, 3, 2):
-            out2(r, k).start()
+        for source in others:
+            out2(r, source).start()
     arrived(y_v.at[pl.ds(0, CHIPS), ONE], out2_r)
     arrived(y_v.at[pl.ds(0, N - 1), TWO], ag3_r)
     for j in range(N):
@@ -365,7 +382,8 @@
         arrived(tsend.at[g, pl.ds(0, N - 1), part], rs_s.at[g])
         arrived(tsend.at[g, pl.ds(0, N - 1), part], ag_s.at[g])
     pair_copy.wait_send()
-    arrived(chips.at[pl.ds(0, CHIPS - 1)], chip_s)
+    arrived(chips.at[pl.ds(0, CHIPS - 1), half], chip_s)
+    arrived(chips.at[pl.ds(0, CHIPS - 1), half], forward_s)
     in2.wait_send()
     arrived(ysum.at[pl.ds(0, CHIPS - 1)], rs2_s)
     arrived(y_v.at[pl.ds(0, N - 1), ONE], out2_s)
@@ -405,8 +423,8 @@
                 vm((N, GROUP, COLS), F32), vm((N, GROUP, COLS), BF16), vm((N, GROUP, COLS), BF16),
                 dma((6,)), dma((SLOTS,)), dma((SLOTS,)), dma((3,)),
                 dma((GROUPS,)), dma((GROUPS,)), dma((GROUPS,)), dma((GROUPS,)),
-                dma, dma, dma, dma,
-                dma, dma, dma, dma((PARTS,)), dma((PARTS,)), dma, dma, dma, dma, dma, dma,
+                dma, dma, dma, dma, dma, dma,
+                dma, dma, dma, dma((PARTS,)), dma((PARTS,)), dma, dma, dma, dma, dma, dma, dma,
             ],
             compiler_params=pltpu.CompilerParams(collective_id=0, has_side_effects=True, vmem_limit_bytes=58_000_000),
             name="layer",

time: 57.9 us -> 57 us (0.984)
  Pallas kernels: 57 us -> 56.1 us
    pallas_call x1, Pallas kernels: 57 us -> 56.1 us  [step(): pl.pallas_call(kernel, out_shape=pltpu.VMEM((ROWS, D), BF16), in_specs=[p...]
where the time goes in v5:
time: 57 us; the launch traced here: 56.8 us
  Pallas kernels  56.1 us (98%)
  local copies, waits for them, and re-layouts  0.75 us (1%)
    pallas_call x1, Pallas kernels, step(): pl.pallas_call(kernel, out_shape=pltpu.VMEM((ROWS, D), BF16), in_specs=[p...  56.1 us

profile of v5, /device:TPU:0, one launch (start us, length us, event | category | flops | bytes accessed | tf_op | source)
XLA Modules:
  0.0 56.8 jit_solution(5768936808158502436)
XLA Ops:
  0.0 56.1 %layer.1 = bf16[64,3072]{1,0:T(8,128)(2,1)S(1)} custom-call(bf16[64,3072]{1,0:T(8,128)(2,1)} %x_h.1, bf16[16,1536,1024]{2,1,0:T(8,128)(2,1)} %bitcast.8, bf16[16,1536,1024]{2,1,0:T(8,128)(2,1)} %bitcast.9, bf16[24,128]{1,0:T(8,128)(2,1)} %bitcast.10, bf16[3072,384]{1,0:T(8,128)(2,1)} %wq_h.1, bf16[384,3072]{1,0:T(8,128)(2,1)} %wo_h.1, ...), custom_call_target="tpu_custom_call" | custom-call | tf_op jit(solution)/shard_map/layer/pallas_call | solution.py:408
  56.1 0.7 %copy.13 = bf16[64,3072]{1,0:T(8,128)(2,1)} copy(bf16[64,3072]{1,0:T(8,128)(2,1)S(1)} %layer.1) | data formatting | bytes 786432

commit v6 on v5

--- a/solution.py
+++ b/solution.py
@@ -25,9 +25,11 @@
 GROUPS = ROWS // GROUP
 EARLY = GROUPS - 1
 HALF = GROUP // 2
+WIDE = 2
+SETS = WIDE + 3
 PER = GROUP // SEQS
 MTILE = 256
-PART = 16
+PART = 48
 PARTS = EARLY * GROUP // PART
 F32, BF16 = jnp.float32, jnp.bfloat16
 
@@ -46,7 +48,7 @@
            a_v, q_s, p_s, seen_s, term_s, tsend, trecv, psend, precv, chips, h_v, hid_v,
            ysend, yrecv, yown, ysum, yfar, y_v, zown, zsend, zrecv,
            in_sem, k_sem, v_sem, w_sem, rs_s, rs_r, ag_s, ag_r, pair_s, pair_r, chip_s, chip_r, forward_s, forward_r,
-           in2_s, in2_r, rs2_s, rs2_r, ag2_r, out2_s, out2_r, rs3_s, rs3_r, ag3_s, ag3_r, out3_r):
+           in2_s, in2_r, rs2_s, rs2_r, ag2_r, out2_s, out2_r, rs3_s, rs3_r, ag3_s, ag3_r):
     me = lax.axis_index("tp")
 
     z, core = me // 2, lax.rem(me, 2)
@@ -162,6 +164,9 @@
 
     FIRST, LAST = (pl.ds(EARLY * GROUP + t * HALF, HALF) for t in range(2))
 
+    def narrow(g):
+        return pl.ds(WIDE * GROUP + (g - WIDE) * HALF, HALF)
+
     def send_terms(g, rows, size):
         term = dot(seen_s[rows, :].astype(BF16), wo_v[...])
         for j in range(N):
@@ -255,17 +260,23 @@
             wo_in.wait()
             gm_in.wait()
 
-        @pl.when(lax.rem(c, PER) == 0)
+        @pl.when(jnp.logical_and(lax.rem(c, PER) == 0, c <= WIDE * PER))
         def _():
             send_terms(c // PER - 1, group_rows(c // PER - 1), GROUP)
 
-        @pl.when(c == CHUNKS - 2)
-        def _():
-            send_terms(EARLY, FIRST, HALF)
-
-        @pl.when(jnp.logical_or(c == CHUNKS - 2, jnp.logical_and(lax.rem(c, PER) == PER - 1, jnp.logical_and(c > PER, c < CHUNKS - 1))))
+        for g in range(WIDE, SETS):
+            @pl.when(c == (g - WIDE) * PER // 2 + WIDE * PER + PER // 2)
+            def _(g=g):
+                send_terms(g, narrow(g), HALF)
+
+        @pl.when(jnp.logical_and(lax.rem(c, PER) == PER - 1, jnp.logical_and(c > PER, c <= WIDE * PER + PER - 1)))
         def _():
             finish_h(c // PER - 1, group_rows(c // PER - 1), GROUP)
+
+        for g, at in ((WIDE, CHUNKS - 3), (WIDE + 1, CHUNKS - 2)):
+            @pl.when(c == at)
+            def _(g=g):
+                finish_h(g, narrow(g), HALF)
 
         return 0
 
@@ -273,10 +284,12 @@
     v_in(CHUNKS - 1).wait()
     values_of(CHUNKS - 1, p_s[...])
     send_pair()
-    finish_h(EARLY, FIRST, HALF)
-    lax.fori_loop(0, EARLY - 1, early_h, 0)
+    finish_h(SETS - 1, FIRST, HALF)
+    lax.fori_loop(0, WIDE, early_h, 0)
     send_chip()
-    early_h(EARLY - 1, 0)
+    for g in (WIDE, WIDE + 1):
+        arrived(h_v.at[pl.ds(0, N - 1), narrow(g)], ag_r.at[g])
+    norm_h(group_rows(WIDE))
 
     ONE, TWO = pl.ds(0, EARLY * GROUP), pl.ds(EARLY * GROUP, GROUP)
 
@@ -346,7 +359,7 @@
             rs2(r, to).start()
     forward_chips()
 
-    arrived(h_v.at[pl.ds(0, N - 1), FIRST], ag_r.at[EARLY])
+    arrived(h_v.at[pl.ds(0, N - 1), FIRST], ag_r.at[SETS - 1])
     last_h()
     norm_h(TWO)
     for n in range(FF // MTILE):
@@ -377,8 +390,8 @@
     for j in range(N):
         out_h[:, j * COLS:(j + 1) * COLS] = y_v[j]
 
-    for g in range(GROUPS):
-        part = pl.ds(0, GROUP if g < EARLY else HALF)
+    for g in range(SETS):
+        part = pl.ds(0, GROUP if g < WIDE else HALF)
         arrived(tsend.at[g, pl.ds(0, N - 1), part], rs_s.at[g])
         arrived(tsend.at[g, pl.ds(0, N - 1), part], ag_s.at[g])
     pair_copy.wait_send()
@@ -415,16 +428,16 @@
                 vm((D, QD), BF16), vm((QD, D), BF16), vm((D, FF), BF16), vm((D, FF), BF16), vm((FF, D), BF16),
                 vm((SLOTS, SEQS * QD, CACHE), BF16), vm((SLOTS, SEQS * QD, CACHE), BF16),
                 vm((ROWS, D), BF16), vm((ROWS, QD), F32), vm((SEQS * HEADS, CACHE), BF16), vm((ROWS, QD), F32),
-                vm((GROUPS, N, GROUP, COLS), F32), vm((GROUPS, N, GROUP, COLS), BF16), vm((GROUPS, N, GROUP, COLS), BF16),
+                vm((SETS, N, GROUP, COLS), F32), vm((SETS, N, GROUP, COLS), BF16), vm((SETS, N, GROUP, COLS), BF16),
                 vm((N, HALF, COLS), BF16), vm((N, HALF, COLS), BF16), vm((CHIPS, N, HALF, COLS), BF16),
                 vm((N, ROWS, COLS), BF16), vm((ROWS, FF), BF16),
                 vm((CHIPS, EARLY * GROUP, COLS), BF16), vm((CHIPS, EARLY * GROUP, COLS), BF16), vm((CHIPS, EARLY * GROUP, COLS), F32),
                 vm((CHIPS, EARLY * GROUP, COLS), BF16), vm((CHIPS, EARLY * GROUP, COLS), BF16), vm((N, ROWS, COLS), BF16),
                 vm((N, GROUP, COLS), F32), vm((N, GROUP, COLS), BF16), vm((N, GROUP, COLS), BF16),
                 dma((6,)), dma((SLOTS,)), dma((SLOTS,)), dma((3,)),
-                dma((GROUPS,)), dma((GROUPS,)), dma((GROUPS,)), dma((GROUPS,)),
+                dma((SETS,)), dma((SETS,)), dma((SETS,)), dma((SETS,)),
                 dma, dma, dma, dma, dma, dma,
-                dma, dma, dma, dma((PARTS,)), dma((PARTS,)), dma, dma, dma, dma, dma, dma, dma,
+                dma, dma, dma, dma((PARTS,)), dma((PARTS,)), dma, dma, dma, dma, dma, dma,
             ],
             compiler_params=pltpu.CompilerParams(collective_id=0, has_side_effects=True, vmem_limit_bytes=58_000_000),
             name="layer",

time: 57 us -> 56.6 us (level)
  no operation moved by 1% of the time
where the time goes in v6:
time: 56.6 us; the launch traced here: 56.5 us
  Pallas kernels  55.7 us (98%)
  local copies, waits for them, and re-layouts  0.75 us (1%)
    pallas_call x1, Pallas kernels, step(): pl.pallas_call(kernel, out_shape=pltpu.VMEM((ROWS, D), BF16), in_specs=[p...  55.7 us

profile of v6, /device:TPU:0, one launch (start us, length us, event | category | flops | bytes accessed | tf_op | source)
XLA Modules:
  0.0 56.5 jit_solution(7787136157324502912)
XLA Ops:
  0.0 55.7 %layer.1 = bf16[64,3072]{1,0:T(8,128)(2,1)S(1)} custom-call(bf16[64,3072]{1,0:T(8,128)(2,1)} %x_h.1, bf16[16,1536,1024]{2,1,0:T(8,128)(2,1)} %bitcast.8, bf16[16,1536,1024]{2,1,0:T(8,128)(2,1)} %bitcast.9, bf16[24,128]{1,0:T(8,128)(2,1)} %bitcast.10, bf16[3072,384]{1,0:T(8,128)(2,1)} %wq_h.1, bf16[384,3072]{1,0:T(8,128)(2,1)} %wo_h.1, ...), custom_call_target="tpu_custom_call" | custom-call | tf_op jit(solution)/shard_map/layer/pallas_call | solution.py:421
  55.7 0.7 %copy.13 = bf16[64,3072]{1,0:T(8,128)(2,1)} copy(bf16[64,3072]{1,0:T(8,128)(2,1)S(1)} %layer.1) | data formatting | bytes 786432
